TPU v7x, 128 devices: a whole 4x4x4 slice. The times are simulated.
128 devices in a mesh: expert: 8 (over x, core), shard: 16 (over z, y).
Axes of the slice: x: 4, y: 4, z: 4, core: 2. Of those that a mesh axis runs over, the one named last changes fastest.
Arguments:
- tokens: bfloat16 [1024, 4096], P(('expert', 'shard')), may hold values from -6 to 6
- router: bfloat16 [4096, 8], replicated, may hold values from -0.09375 to 0.09375
- expert_ids: int32 [1024, 2], P(('expert', 'shard')), may hold values from 0 to 7, as said below
- w_gate: bfloat16 [8, 4096, 14336], P('expert', None, 'shard'), may hold values from -0.09375 to 0.09375
- w_up: bfloat16 [8, 4096, 14336], P('expert', None, 'shard'), may hold values from -0.09375 to 0.09375
- w_down: bfloat16 [8, 14336, 4096], P('expert', 'shard'), may hold values from -0.046875 to 0.046875
Outputs:
- mixed: bfloat16 [1024, 4096], P(('expert', 'shard'))
Inputs may be any that keep to these rules, and one draw needn't show every extreme that they name: `expert_ids`: each row names 2 different experts. Within the rows of one device no expert is named more than 4 times, and on every device some expert is named exactly 4 times.
All inputs are finite; a program needn't handle non-finite values.
Results may differ from a plain program's by a relative error of at most 0.0074.
Values may be sent and summed in bfloat16 or wider, within the bound.
A program may use at most 128 MiB of HBM per device.

v0:
```python
import jax
import jax.numpy as jnp
from jax import lax
from jax.sharding import PartitionSpec as P


def from_behind(value, axis, steps):
    count = lax.axis_size(axis)
    pairs = [(source, (source + steps) % count) for source in range(count)]
    return lax.ppermute(value, axis, pairs)


def laid_out(blocks, dim):
    blocks = jnp.moveaxis(blocks, 0, dim)
    dims = blocks.shape
    return blocks.reshape(*dims[:dim], dims[dim] * dims[dim + 1], *dims[dim + 2 :])


def work_in_pieces(x, axis, dim, apply, out_dim):
    devices, extent = (lax.axis_size(axis), x.shape[dim])
    count = 2 if extent % 2 == 0 else 1
    gathered, length = ([], extent // count)
    for k in range(count):
        share = lax.slice_in_dim(x, k * length, (k + 1) * length, axis=dim)
        starts = jnp.arange(devices) * extent + k * length
        gathered.append(jax.vmap(apply)(lax.all_gather(share, axis), starts))
    return laid_out(jnp.concatenate(gathered, axis=out_dim + 1), out_dim)


def split_up(x, dim, devices):
    before, after = (x.shape[:dim], x.shape[dim + 1 :])
    return jnp.moveaxis(x.reshape(*before, devices, -1, *after), dim, 0)


def sum_at_owner(x, axis, dim):
    devices = lax.axis_size(axis)
    blocks = lax.all_to_all(split_up(x, dim, devices), axis, 0, 0, tiled=True)
    return jnp.sum(blocks.astype(jnp.float32), axis=0)


def shards(tokens, router, expert_ids, w_gate, w_up, w_down):
    local_tokens = tokens.shape[0]
    width = tokens.shape[1]
    n_experts = router.shape[1]
    slots_per = local_tokens // 2
    half_slots = slots_per // 2
    shadow_gate, shadow_up, shadow_down = from_behind((w_gate, w_up, w_down), "expert", -1)
    logits = jnp.dot(tokens, router, preferred_element_type=jnp.float32)
    chosen = jnp.take_along_axis(logits, expert_ids, axis=1)
    first = 1.0 / (1.0 + jnp.exp(-(chosen[:, 0] - chosen[:, 1])))
    gates = jnp.stack([first, 1.0 - first], axis=1)
    flat_ids = expert_ids.reshape(-1)
    onehot = (flat_ids[:, None] == jnp.arange(n_experts, dtype=jnp.int32)[None, :]).astype(
        jnp.int32
    )
    before = jnp.cumsum(onehot, axis=0) - onehot
    slots = jnp.sum(before * onehot, axis=1)
    positions = flat_ids * slots_per + slots
    token_index = jnp.repeat(jnp.arange(local_tokens, dtype=jnp.int32), expert_ids.shape[1])
    outgoing = jnp.zeros((n_experts * slots_per, width), jnp.bfloat16)
    outgoing = outgoing.at[positions].set(tokens[token_index])
    outgoing = outgoing.reshape(n_experts, half_slots, 2, width)
    even_rows = outgoing[:, :, 0]
    odd_rows = jnp.roll(outgoing[:, :, 1], -1, axis=0)
    sending = jnp.stack([even_rows, odd_rows], axis=0)
    arrived = lax.all_to_all(sending, "expert", split_axis=1, concat_axis=1, tiled=True)
    arrived = arrived.reshape(2, n_experts * half_slots, width)
    gate_w = w_gate[0]
    up_w = w_up[0]
    down_w = w_down[0]
    gate_s = shadow_gate[0]
    up_s = shadow_up[0]
    down_s = shadow_down[0]

    def swiglu(rows, gate_m, up_m):
        gate = jnp.dot(rows, gate_m, preferred_element_type=jnp.float32)
        up = jnp.dot(rows, up_m, preferred_element_type=jnp.float32)
        return (jax.nn.silu(gate) * up).astype(jnp.bfloat16)

    def hidden_rows(piece, start):
        own = swiglu(piece[0], gate_w, up_w)
        other = swiglu(piece[1], gate_s, up_s)
        return jnp.stack([own, other], axis=1)

    hidden = work_in_pieces(arrived, "shard", 1, hidden_rows, 0)
    own = jnp.dot(hidden[:, 0], down_w, preferred_element_type=jnp.float32)
    other = jnp.dot(hidden[:, 1], down_s, preferred_element_type=jnp.float32)
    summed = sum_at_owner(jnp.stack([own, other], axis=1).astype(jnp.bfloat16), "shard", 0)
    finished = summed.astype(jnp.bfloat16).reshape(n_experts, half_slots, 2, width)
    returned = lax.all_to_all(finished, "expert", split_axis=0, concat_axis=0, tiled=True)
    even_back = returned[:, :, 0]
    odd_back = jnp.roll(returned[:, :, 1], 1, axis=0)
    by_expert = jnp.stack([even_back, odd_back], axis=2).reshape(n_experts * slots_per, width)
    picked = (
        by_expert[positions].reshape(local_tokens, expert_ids.shape[1], width).astype(jnp.float32)
    )
    mixed = jnp.sum(gates[:, :, None] * picked, axis=1)
    return mixed.astype(jnp.bfloat16)


def solution(mesh):
    placed = (
        P(("expert", "shard"), None),
        P(),
        P(("expert", "shard"), None),
        P("expert", None, "shard"),
        P("expert", None, "shard"),
        P("expert", "shard", None),
    )
    return jax.shard_map(
        shards, mesh=mesh, in_specs=placed, out_specs=P(("expert", "shard"), None), check_vma=False
    )
```

profile of v0, /device:TPU:0, one launch (start us, length us, event | category | flops | bytes accessed | tf_op | source)
XLA Modules:
  0.0 370.3 jit_solution(15408557589807152107)
XLA Ops:
  6.5 0.7 broadcast_multiply_fusion
  7.3 0.8 copy.103
  8.7 1.2 scatter_custom_fusion
  11.1 11.7 %all_to_all.15 = bf16[2,8,2,4096]{3,2,0,1:T(2,128)(2,1)S(1)} all-to-all(bf16[2,8,2,4096]{3,2,0,1:T(2,128)(2,1)S(1)} %copy.113), channel_id=1, replica_groups=mesh['expert'=8,'shard'=16] {'expert'}, dimensions={1} | all-to-all | bytes 524288 | tf_op jit(solution)/shard_map/all_to_all | solution.py:66
  23.3 0.7 copy.118
  24.5 1.0 collective-permute-start.1
  25.6 0.7 copy.115
  26.4 43.4 %all-gather.7.cloned.1.call-done = bf16[32,8,4096]{2,1,0:T(8,128)(2,1)} async-done(((bf16[2,8,4096]{2,1,0:T(8,128)(2,1)}), bf16[32,8,4096]{2,1,0:T(8,128)(2,1)}) %all-gather.7.cloned.1.call-update) | async-done | bytes 2097168 | tf_op jit(solution)/shard_map/all_gather | solution.py:26
  69.8 4.7 %fusion.16 = f32[16,8,896]{2,1,0:T(8,128)S(1)} fusion(bf16[1,4096,896]{2,1,0:T(8,128)(2,1)} %param.9, bf16[16,2,8,4096]{3,2,1,0:T(8,128)(2,1)} %bitcast.140), kind=kOutput, calls=%fused_computation.20 | convolution fusion | flops 939524096 | bytes 8847360 | tf_op jit(solution)/shard_map/vmap()/dot_general | solution.py:76
  74.5 41.8 %all-gather.5.cloned.1.call-done = bf16[32,8,4096]{2,1,0:T(8,128)(2,1)} async-done(((bf16[2,8,4096]{2,1,0:T(8,128)(2,1)}), bf16[32,8,4096]{2,1,0:T(8,128)(2,1)}) %all-gather.5.cloned.1.call-update) | async-done | bytes 2097168 | tf_op jit(solution)/shard_map/all_gather | solution.py:26
  116.2 4.8 %fusion.18 = f32[16,8,896]{2,1,0:T(8,128)S(1)} fusion(bf16[1,4096,896]{2,1,0:T(8,128)(2,1)} %param.9, bf16[16,2,8,4096]{3,2,1,0:T(8,128)(2,1)} %bitcast.144), kind=kOutput, calls=%fused_computation.22 | convolution fusion | flops 939524096 | bytes 8847360 | tf_op jit(solution)/shard_map/vmap()/dot_general | solution.py:76
  121.1 4.5 %fusion.47 = bf16[16,8,1,896]{3,1,0,2:T(8,128)(2,1)S(1)} fusion(bf16[1,4096,896]{2,1,0:T(8,128)(2,1)} %param.10, bf16[16,2,8,4096]{3,2,1,0:T(8,128)(2,1)S(1)} %bitcast.141, f32[16,8,896]{2,1,0:T(8,128)S(1)} %fusion.16), kind=kOutput, calls=%fused_computation.34 | convolution fusion | flops 940212224 | bytes 9076736 | tf_op jit(solution)/shard_map/vmap()/dot_general | solution.py:77
  125.8 1.3 fusion.44
  127.1 4.4 %fusion.8 = f32[16,8,896]{2,1,0:T(8,128)S(1)} fusion(bf16[1,4096,896]{2,1,0:T(8,128)(2,1)} %collective-permute-done, bf16[16,2,8,4096]{3,2,1,0:T(8,128)(2,1)S(1)} %bitcast.142), kind=kOutput, calls=%fused_computation.12 | convolution fusion | flops 939524096 | bytes 8847360 | tf_op jit(solution)/shard_map/vmap()/dot_general | solution.py:76
  131.4 4.4 %fusion.10 = f32[16,8,896]{2,1,0:T(8,128)S(1)} fusion(bf16[1,4096,896]{2,1,0:T(8,128)(2,1)} %collective-permute-done, bf16[16,2,8,4096]{3,2,1,0:T(8,128)(2,1)S(1)} %bitcast.146), kind=kOutput, calls=%fused_computation.14 | convolution fusion | flops 939524096 | bytes 8847360 | tf_op jit(solution)/shard_map/vmap()/dot_general | solution.py:76
  135.8 47.4 %collective-permute-done.1 = bf16[1,4096,896]{2,1,0:T(8,128)(2,1)} collective-permute-done((bf16[1,4096,896]{2,1,0:T(8,128)(2,1)}, bf16[1,4096,896]{2,1,0:T(8,128)(2,1)}, u32[]{:S(2)}, u32[]{:S(2)}) %collective-permute-start.1) | collective-permute-done | bytes 7340064 | tf_op jit(solution)/shard_map/ppermute | solution.py:10
  183.2 4.5 %fusion.51 = bf16[16,8,1,896]{3,1,0,2:T(8,128)(2,1)S(1)} fusion(f32[16,8,896]{2,1,0:T(8,128)S(1)} %fusion.8, bf16[1,4096,896]{2,1,0:T(8,128)(2,1)} %collective-permute-done.1, bf16[16,2,8,4096]{3,2,1,0:T(8,128)(2,1)S(1)} %bitcast.143), kind=kOutput, calls=%fused_computation.46 | convolution fusion | flops 940212224 | bytes 9076736 | tf_op jit(solution)/shard_map/vmap()/dot_general | solution.py:77
  187.8 4.5 %fusion.50 = bf16[16,8,1,896]{3,1,0,2:T(8,128)(2,1)S(1)} fusion(f32[16,8,896]{2,1,0:T(8,128)S(1)} %fusion.10, bf16[1,4096,896]{2,1,0:T(8,128)(2,1)} %collective-permute-done.1, bf16[16,2,8,4096]{3,2,1,0:T(8,128)(2,1)S(1)} %bitcast.147), kind=kOutput, calls=%fused_computation.45 | convolution fusion | flops 940212224 | bytes 9076736 | tf_op jit(solution)/shard_map/vmap()/dot_general | solution.py:77
  192.5 2.6 fusion.29
  195.2 66.7 %collective-permute-done.2 = bf16[1,896,4096]{2,1,0:T(8,128)(2,1)} collective-permute-done((bf16[1,896,4096]{2,1,0:T(8,128)(2,1)}, bf16[1,896,4096]{2,1,0:T(8,128)(2,1)}, u32[]{:S(2)}, u32[]{:S(2)}) %collective-permute-start.2) | collective-permute-done | bytes 7340064 | tf_op jit(solution)/shard_map/ppermute | solution.py:10
  261.9 5.5 %fusion.26 = bf16[16,16,1,4096]{3,1,0,2:T(8,128)(2,1)S(1)} fusion(bf16[16,16,896]{2,1,0:T(8,128)(2,1)S(1)} %bitcast.153, bf16[1,896,4096]{2,1,0:T(8,128)(2,1)} %collective-permute-done.2), kind=kOutput, calls=%fused_computation.26 | convolution fusion | flops 1880096768 | bytes 9895936 | tf_op jit(solution)/shard_map/dot_general | solution.py:87
  267.8 2.2 copy.121
  270.0 8.2 %all-to-all-start.1 = ((bf16[16,16,2,4096]{3,1,2,0:T(8,128)(2,1)}), bf16[16,16,2,4096]{3,1,2,0:T(8,128)(2,1)}, u32[]{:S(2)}, u32[]{:S(2)}) async-start(bf16[16,16,2,4096]{3,1,2,0:T(8,128)(2,1)} %copy.121), calls=%async_computation.1 | async-start | bytes 8388608 | tf_op jit(solution)/shard_map/all_to_all | solution.py:37
  278.7 0.7 gather_fusion.1
  279.4 65.7 %all-to-all-done.1 = bf16[16,16,2,4096]{3,1,2,0:T(8,128)(2,1)} async-done(((bf16[16,16,2,4096]{3,1,2,0:T(8,128)(2,1)}), bf16[16,16,2,4096]{3,1,2,0:T(8,128)(2,1)}, u32[]{:S(2)}, u32[]{:S(2)}) %all-to-all-start.1) | async-done | bytes 4194336 | tf_op jit(solution)/shard_map/all_to_all | solution.py:37
  345.1 3.0 reduce_sum.34
  348.1 1.0 copy.123
  349.1 3.4 all-to-all-start.2
  352.7 7.3 %all-to-all-done.2 = bf16[8,2,2,4096]{3,2,1,0:T(2,128)(2,1)S(1)} async-done(((bf16[8,2,2,4096]{3,2,1,0:T(2,128)(2,1)}), bf16[8,2,2,4096]{3,2,1,0:T(2,128)(2,1)S(1)}, u32[]{:S(2)}, u32[]{:S(2)}) %all-to-all-start.2) | async-done | bytes 262176 | tf_op jit(solution)/shard_map/all_to_all | solution.py:90
  360.9 0.6 pad_maximum_fusion.2
  361.6 0.6 gather_fusion
  362.4 1.0 multiply_reduce_fusion
  (68 shorter events, 5.3 us)
Async XLA Ops:
  6.5 2.1 copy-start
  6.5 63.3 %all-gather.7.cloned.1.call-start = ((), (), s32[]{:S(2)}) async-start(), calls=%async_computation.4 | async-start | bytes 2228224 | tf_op jit(solution)/shard_map/all_gather | solution.py:26
  24.1 92.2 %all-gather.5.cloned.1.call-start = ((), (), s32[]{:S(2)}) async-start(), calls=%async_computation.3 | async-start | bytes 2228224 | tf_op jit(solution)/shard_map/all_gather | solution.py:26
  24.3 102.8 %collective-permute-start = (bf16[1,4096,896]{2,1,0:T(8,128)(2,1)}, bf16[1,4096,896]{2,1,0:T(8,128)(2,1)}, u32[]{:S(2)}, u32[]{:S(2)}) collective-permute-start(bf16[1,4096,896]{2,1,0:T(8,128)(2,1)} %param.9), channel_id=1, source_target_pairs={{0,112},{16,0},{32,16},{48,32},{64,48},{80,64},{96,80},{112,96},{1... | collective-permute-start | bytes 22020104 | tf_op jit(solution)/shard_map/ppermute | solution.py:10
  24.5 158.7 %collective-permute-start.1 = (bf16[1,4096,896]{2,1,0:T(8,128)(2,1)}, bf16[1,4096,896]{2,1,0:T(8,128)(2,1)}, u32[]{:S(2)}, u32[]{:S(2)}) collective-permute-start(bf16[1,4096,896]{2,1,0:T(8,128)(2,1)} %param.10), channel_id=1, source_target_pairs={{0,112},{16,0},{32,16},{48,32},{64,48},{80,64},{96,80},{112,96},{1... | collective-permute-start | bytes 22020104 | tf_op jit(solution)/shard_map/ppermute | solution.py:10
  26.4 235.5 %collective-permute-start.2 = (bf16[1,896,4096]{2,1,0:T(8,128)(2,1)}, bf16[1,896,4096]{2,1,0:T(8,128)(2,1)}, u32[]{:S(2)}, u32[]{:S(2)}) collective-permute-start(bf16[1,896,4096]{2,1,0:T(8,128)(2,1)} %param.11), channel_id=1, source_target_pairs={{0,112},{16,0},{32,16},{48,32},{64,48},{80,64},{96,80},{112,96},{1... | collective-permute-start | bytes 22020104 | tf_op jit(solution)/shard_map/ppermute | solution.py:10
  116.2 4.8 %copy-start.1 = (bf16[32,8,4096]{2,1,0:T(8,128)(2,1)S(1)}, bf16[32,8,4096]{2,1,0:T(8,128)(2,1)}, u32[]{:S(2)}) copy-start(bf16[32,8,4096]{2,1,0:T(8,128)(2,1)} %all-gather.7.cloned.1.call-done) | copy-start | bytes 6291460
  116.2 9.4 %slice-start = ((s8[7340032]{0:T(1024)(128)(4,1)}), s8[4194304]{0:T(1024)(128)(4,1)S(1)}, s32[]{:S(2)}) async-start(s8[7340032]{0:T(1024)(128)(4,1)} %bitcast.157), calls=%async_computation.5 | async-start | bytes 8388608
  121.1 4.6 %copy-start.2 = (bf16[32,8,4096]{2,1,0:T(8,128)(2,1)S(1)}, bf16[32,8,4096]{2,1,0:T(8,128)(2,1)}, u32[]{:S(2)}) copy-start(bf16[32,8,4096]{2,1,0:T(8,128)(2,1)} %all-gather.5.cloned.1.call-done) | copy-start | bytes 6291460
  121.1 4.7 %slice-start.1 = ((s8[7340032]{0:T(1024)(128)(4,1)}), s8[3145728]{0:T(1024)(128)(4,1)S(1)}, s32[]{:S(2)}) async-start(s8[7340032]{0:T(1024)(128)(4,1)} %bitcast.157), calls=%async_computation.6 | async-start | bytes 6291456
  183.2 9.3 %slice-start.2 = ((s8[7340032]{0:T(1024)(128)(4,1)}), s8[4194304]{0:T(1024)(128)(4,1)S(1)}, s32[]{:S(2)}) async-start(s8[7340032]{0:T(1024)(128)(4,1)} %bitcast.159), calls=%async_computation.7 | async-start | bytes 8388608
  187.8 4.7 %slice-start.3 = ((s8[7340032]{0:T(1024)(128)(4,1)}), s8[3145728]{0:T(1024)(128)(4,1)S(1)}, s32[]{:S(2)}) async-start(s8[7340032]{0:T(1024)(128)(4,1)} %bitcast.159), calls=%async_computation.8 | async-start | bytes 6291456
  270.0 8.5 %copy-start.3 = (bf16[4096,8]{0,1:T(8,128)(2,1)S(1)}, bf16[4096,8]{0,1:T(8,128)(2,1)}, u32[]{:S(2)}) copy-start(bf16[4096,8]{0,1:T(8,128)(2,1)} %param.7) | copy-start | bytes 196612
  270.0 75.1 %all-to-all-start.1 = ((bf16[16,16,2,4096]{3,1,2,0:T(8,128)(2,1)}), bf16[16,16,2,4096]{3,1,2,0:T(8,128)(2,1)}, u32[]{:S(2)}, u32[]{:S(2)}) async-start(bf16[16,16,2,4096]{3,1,2,0:T(8,128)(2,1)} %copy.121), calls=%async_computation.1 | async-start | bytes 8388608 | tf_op jit(solution)/shard_map/all_to_all | solution.py:37
  349.1 10.8 %all-to-all-start.2 = ((bf16[8,2,2,4096]{3,2,1,0:T(2,128)(2,1)}), bf16[8,2,2,4096]{3,2,1,0:T(2,128)(2,1)S(1)}, u32[]{:S(2)}, u32[]{:S(2)}) async-start(bf16[8,2,2,4096]{3,2,1,0:T(2,128)(2,1)} %bitcast.36), calls=%async_computation.2 | async-start | bytes 524288 | tf_op jit(solution)/shard_map/all_to_all | solution.py:90
Sparse Core Ops, SparseCore 0:
  24.2 45.5 all-gather.6
  71.9 44.2 all-gather.4
where the time goes:
time: 371 us; the launch traced here: 370 us
  waiting for transfers between devices  272 us (73%)
  matrix products  41.4 us (11%)
  between operations  13.8 us (4%)
  starting transfers between devices  13.2 us (4%)
  blocking collectives  11.7 us (3%)
  local copies, waits for them, and re-layouts  11.3 us (3%)
  other arithmetic  6.56 us (2%)
    ppermute x3, waiting for transfers between devices, from_behind(): return lax.ppermute(value, axis, pairs)  114 us
    all_gather x2, waiting for transfers between devices, work_in_pieces(): gathered.append(jax.vmap(apply)(lax.all_gather(share, axis), starts))  85.2 us
    all_to_all x1, waiting for transfers between devices, sum_at_owner(): blocks = lax.all_to_all(split_up(x, dim, devices), axis, 0, 0, tiled=True)  65.7 us
    dot_general x4, matrix products, swiglu(): gate = jnp.dot(rows, gate_m, preferred_element_type=jnp.float32)  18.2 us
    dot_general x4, matrix products, swiglu(): up = jnp.dot(rows, up_m, preferred_element_type=jnp.float32)  14.9 us
    all_to_all x1, blocking collectives, shards(): lax.all_to_all(sending, 'expert', split_axis=1, concat_axis=1, tiled=True)  11.7 us
    all_to_all x1, starting transfers between devices, sum_at_owner(): blocks = lax.all_to_all(split_up(x, dim, devices), axis, 0, 0, tiled=True)  8.23 us
  transfers between devices with their start and end apart: 7, of which 6 were waited for; matrix products, arithmetic and copies ran while one was open for 10% of the time, Pallas kernels for 0%

commit v1 on v0

v1 whole, which is shorter than its diff:
```python
import jax
import jax.numpy as jnp
from jax import lax
from jax.sharding import PartitionSpec as P


def split_up(x, dim, devices):
    before, after = (x.shape[:dim], x.shape[dim + 1 :])
    return jnp.moveaxis(x.reshape(*before, devices, -1, *after), dim, 0)


def sum_at_owner(x, axis, dim):
    devices = lax.axis_size(axis)
    blocks = lax.all_to_all(split_up(x, dim, devices), axis, 0, 0, tiled=True)
    return jnp.sum(blocks.astype(jnp.float32), axis=0)


def shards(tokens, router, expert_ids, w_gate, w_up, w_down):
    local_tokens = tokens.shape[0]
    width = tokens.shape[1]
    n_experts = router.shape[1]
    slots_per = local_tokens // 2
    logits = jnp.dot(tokens, router, preferred_element_type=jnp.float32)
    lane = jnp.arange(n_experts * slots_per, dtype=jnp.int32)[None, :]
    lane_expert, lane_slot = lane // slots_per, lane % slots_per
    names = [expert_ids[:, k : k + 1] == lane_expert for k in range(expert_ids.shape[1])]
    named = (names[0] | names[1]).astype(jnp.int32)
    before = jnp.cumsum(named, axis=0) - named
    placed = [name & (before == lane_slot) for name in names]
    chosen = [
        jnp.sum(jnp.where(expert_ids[:, k : k + 1] == jnp.arange(n_experts)[None, :], logits, 0.0), axis=1, keepdims=True)
        for k in range(2)
    ]
    first = 1.0 / (1.0 + jnp.exp(-(chosen[0] - chosen[1])))
    gates = [first, 1.0 - first]
    pick = (placed[0] | placed[1]).astype(jnp.bfloat16)
    outgoing = jnp.einsum("ts,td->sd", pick, tokens).astype(jnp.bfloat16)
    outgoing = outgoing.reshape(n_experts, slots_per, width)
    arrived = lax.all_to_all(outgoing, "expert", split_axis=0, concat_axis=0, tiled=True)
    arrived = arrived.reshape(n_experts * slots_per, width)
    rows = lax.all_gather(arrived, "shard", tiled=True)
    gate = jnp.dot(rows, w_gate[0], preferred_element_type=jnp.float32)
    up = jnp.dot(rows, w_up[0], preferred_element_type=jnp.float32)
    hidden = (jax.nn.silu(gate) * up).astype(jnp.bfloat16)
    part = jnp.dot(hidden, w_down[0], preferred_element_type=jnp.float32).astype(jnp.bfloat16)
    summed = sum_at_owner(part, "shard", 0)
    finished = summed.astype(jnp.bfloat16).reshape(n_experts, slots_per, width)
    returned = lax.all_to_all(finished, "expert", split_axis=0, concat_axis=0, tiled=True)
    returned = returned.reshape(n_experts * slots_per, width)
    mix = sum(jnp.where(p, g, 0.0) for p, g in zip(placed, gates))
    mixed = jnp.dot(mix, returned.astype(jnp.float32), precision=lax.Precision.HIGHEST)
    return mixed.astype(jnp.bfloat16)


def solution(mesh):
    placed = (
        P(("expert", "shard"), None),
        P(),
        P(("expert", "shard"), None),
        P("expert", None, "shard"),
        P("expert", None, "shard"),
        P("expert", "shard", None),
    )
    return jax.shard_map(
        shards, mesh=mesh, in_specs=placed, out_specs=P(("expert", "shard"), None), check_vma=False
    )
```

time: 371 us -> 179 us (0.48)
  waiting for transfers between devices: 272 us -> 59.5 us
  blocking collectives: 11.7 us -> 67.8 us
  matrix products: 41.4 us -> 27.9 us
  starting transfers between devices: 13.2 us -> 4.26 us
  local copies, waits for them, and re-layouts: 11.3 us -> 2.48 us
    ppermute x3 -> x0, waiting for transfers between devices: 114 us -> none  [from_behind(): return lax.ppermute(value, axis, pairs)]
    all_to_all x1 -> x0, waiting for transfers between devices: 65.7 us -> none  [sum_at_owner(): blocks = lax.all_to_all(split_up(x, dim, devices), axis, 0, 0, tiled=True)]
    all_to_all x1 -> x2, blocking collectives: 11.7 us -> 67.8 us  [the longest x1 56.1 us: sum_at_owner(): blocks = lax.all_to_all(split_up(x, dim, devices), axis, 0, 0, tiled=True)]
    all_gather x2 -> x1, waiting for transfers between devices: 85.2 us -> 52.2 us  [shards(): rows = lax.all_gather(arrived, 'shard', tiled=True)]
    dot_general x10 -> x4, matrix products: 41.2 us -> 27.7 us  [the longest x1 16.4 us: shards(): jnp.dot(hidden, w_down[0], preferred_element_type=jnp.float32)]
    all_to_all x1 -> x0, starting transfers between devices: 8.23 us -> none  [sum_at_owner(): blocks = lax.all_to_all(split_up(x, dim, devices), axis, 0, 0, tiled=True)]
  transfers between devices with their start and end apart: 7 -> 2, of which waited for: 6 -> 2; matrix products, arithmetic and copies ran while one was open for 10% -> 0% of each run, Pallas kernels for 0% -> 0%
where the time goes in v1:
time: 179 us
  blocking collectives  67.8 us (38%)
  waiting for transfers between devices  59.5 us (33%)
  matrix products  27.9 us (16%)
  between operations  13.4 us (7%)
  starting transfers between devices  4.26 us (2%)
  other arithmetic  3.13 us (2%)
  local copies, waits for them, and re-layouts  2.48 us (1%)
    all_to_all x1, blocking collectives, sum_at_owner(): blocks = lax.all_to_all(split_up(x, dim, devices), axis, 0, 0, tiled=True)  56.1 us
    all_gather x1, waiting for transfers between devices, shards(): rows = lax.all_gather(arrived, 'shard', tiled=True)  52.2 us
    dot_general x1, matrix products, shards(): jnp.dot(hidden, w_down[0], preferred_element_type=jnp.float32)  16.4 us
    all_to_all x1, blocking collectives, shards(): lax.all_to_all(outgoing, 'expert', split_axis=0, concat_axis=0, tiled=True)  11.7 us
    dot_general x1, matrix products, shards(): gate = jnp.dot(rows, w_gate[0], preferred_element_type=jnp.float32)  10.1 us
    all_to_all x1, waiting for transfers between devices, shards(): lax.all_to_all(finished, 'expert', split_axis=0, concat_axis=0, tiled=True)  7.33 us
    all_to_all x1, starting transfers between devices, shards(): lax.all_to_all(finished, 'expert', split_axis=0, concat_axis=0, tiled=True)  4.25 us
  transfers between devices with their start and end apart: 2, of which 2 were waited for; matrix products, arithmetic and copies ran while one was open for 0% of the time, Pallas kernels for 0%

profile of v1, /device:TPU:0, one launch (start us, length us, event | category | flops | bytes accessed | tf_op | source)
XLA Modules:
  0.0 178.5 jit_solution(7834744182151370400)
XLA Ops:
  6.5 0.0 copy-start
  6.5 0.0 all-gather.2.cloned.1.call-start
  6.5 0.8 slice_bitcast_fusion.1
  7.3 0.1 fusion.16
  7.4 0.0 copy-done
  7.4 0.3 fusion.17
  7.8 0.1 reshape.87
  7.9 11.7 %all_to_all.15 = bf16[8,4,4096]{2,1,0:T(4,128)(2,1)S(1)} all-to-all(bf16[8,4,4096]{2,1,0:T(4,128)(2,1)S(1)} %reshape.87), channel_id=1, replica_groups=mesh['expert'=8,'shard'=16] {'expert'}, dimensions={0} | all-to-all | bytes 524288 | tf_op jit(solution)/shard_map/all_to_all | solution.py:39
  19.6 0.8 reshape.88
  20.3 0.0 all-gather.2.cloned.1.call-update
  20.4 52.2 %all-gather.2.cloned.1.call-done = bf16[512,4096]{1,0:T(8,128)(2,1)} async-done(((bf16[32,4096]{1,0:T(8,128)(2,1)}), bf16[512,4096]{1,0:T(8,128)(2,1)}) %all-gather.2.cloned.1.call-update) | async-done | bytes 4194320 | tf_op jit(solution)/shard_map/all_gather | solution.py:41
  72.6 10.1 %fusion.4 = f32[512,896]{1,0:T(8,128)S(1)} fusion(bf16[512,4096]{1,0:T(8,128)(2,1)} %all-gather.2.cloned.1.call-done, bf16[1,4096,896]{2,1,0:T(8,128)(2,1)} %param.9), kind=kOutput, calls=%fused_computation.4 | convolution fusion | flops 3758096384 | bytes 13369344 | tf_op jit(solution)/shard_map/dot_general | solution.py:42
  82.6 16.4 %fusion.6 = bf16[512,4096]{1,0:T(8,128)(2,1)} fusion(bf16[1,896,4096]{2,1,0:T(8,128)(2,1)} %param.11, f32[512,896]{1,0:T(8,128)S(1)} %fusion.4, bf16[512,4096]{1,0:T(8,128)(2,1)} %all-gather.2.cloned.1.call-done, bf16[1,4096,896]{2,1,0:T(8,128)(2,1)} %param.10), kind=kOutput, calls=%fused_computation.6 | convolution fusion | flops 7521042432 | bytes 24903680 | tf_op jit(solution)/shard_map/dot_general | solution.py:45
  99.0 56.1 %all_to_all.16 = bf16[16,32,4096]{2,1,0:T(8,128)(2,1)} all-to-all(bf16[16,32,4096]{2,1,0:T(8,128)(2,1)} %bitcast.26), channel_id=1, replica_groups=mesh['expert'=8,'shard'=16] {'shard'}, dimensions={0} | all-to-all | bytes 8388608 | tf_op jit(solution)/shard_map/all_to_all | solution.py:14
  155.1 0.0 copy-start.1
  155.1 3.0 %reduce_sum.32 = bf16[32,4096]{1,0:T(8,128)(2,1)S(1)} reduce(bf16[16,32,4096]{2,1,0:T(8,128)(2,1)} %all_to_all.16, bf16[]{:T(256)} %constant.41.clone.1), dimensions={0}, to_apply=%region_3.4 | reduce | flops 1966080 | bytes 4456450 | tf_op jit(solution)/shard_map/reduce_sum | solution.py:15
  158.1 0.8 reshape.90
  158.9 4.3 %all-to-all-start.2 = ((bf16[8,4,4096]{2,1,0:T(4,128)(2,1)}), bf16[8,4,4096]{2,1,0:T(4,128)(2,1)S(1)}, u32[]{:S(2)}, u32[]{:S(2)}) async-start(bf16[8,4,4096]{2,1,0:T(4,128)(2,1)} %reshape.90), calls=%async_computation.2 | async-start | bytes 524288 | tf_op jit(solution)/shard_map/all_to_all | solution.py:48
  163.2 0.0 copy-done.1
  163.2 0.2 select_reduce_fusion
  163.3 7.3 %all-to-all-done.2 = bf16[8,4,4096]{2,1,0:T(4,128)(2,1)S(1)} async-done(((bf16[8,4,4096]{2,1,0:T(4,128)(2,1)}), bf16[8,4,4096]{2,1,0:T(4,128)(2,1)S(1)}, u32[]{:S(2)}, u32[]{:S(2)}) %all-to-all-start.2) | async-done | bytes 262176 | tf_op jit(solution)/shard_map/all_to_all | solution.py:48
  170.7 0.1 reshape.91
  170.7 0.9 convolution_convert_fusion
  (3 shorter events, 0.0 us)
Async XLA Ops:
  6.5 0.9 copy-start
  6.5 66.0 %all-gather.2.cloned.1.call-start = ((), (), s32[]{:S(2)}) async-start(), calls=%async_computation.3 | async-start | bytes 4456448 | tf_op jit(solution)/shard_map/all_gather | solution.py:41
  155.1 8.1 %copy-start.1 = (bf16[4096,8]{0,1:T(8,128)(2,1)S(1)}, bf16[4096,8]{0,1:T(8,128)(2,1)}, u32[]{:S(2)}) copy-start(bf16[4096,8]{0,1:T(8,128)(2,1)} %param.7) | copy-start | bytes 196612
  158.9 11.8 %all-to-all-start.2 = ((bf16[8,4,4096]{2,1,0:T(4,128)(2,1)}), bf16[8,4,4096]{2,1,0:T(4,128)(2,1)S(1)}, u32[]{:S(2)}, u32[]{:S(2)}) async-start(bf16[8,4,4096]{2,1,0:T(4,128)(2,1)} %reshape.90), calls=%async_computation.2 | async-start | bytes 524288 | tf_op jit(solution)/shard_map/all_to_all | solution.py:48
Sparse Core Ops, SparseCore 0:
  20.5 52.0 all-gather.1

commit v2 on v1

v2 whole, which is shorter than its diff:
```python
import functools

import jax
import jax.numpy as jnp
from jax import lax
from jax.experimental import pallas as pl
from jax.experimental.pallas import tpu as pltpu
from jax.sharding import PartitionSpec as P

MESH = pl.DeviceIdType.MESH
BF16, F32 = jnp.bfloat16, jnp.float32
ALL = slice(None)

SIDE = 4
HALF = 2048
INFO = 128
GATHER_PARTS = ((0, 768), (768, 768), (1536, 512 + INFO))
SUM_PARTS = ((0, 768), (768, 768), (1536, 512))
ORDERS = ((0, 1, 2), (1, 2, 0), (2, 0, 1))
TILE = 256


def nt_dot(a, b):
    return lax.dot_general(a, b, (((1,), (1,)), ((), ())), preferred_element_type=F32)


def dot(a, b):
    return jnp.dot(a, b, preferred_element_type=F32)


class Place:
    def __init__(self):
        expert, shard = lax.axis_index("expert"), lax.axis_index("shard")
        self.expert = expert
        self.core = expert % 2
        self.own = (expert // 2, shard // SIDE, shard % SIDE)

    def device(self, dim=None, step=0, core=None):
        x, z, y = (
            lax.rem(v + step, SIDE) if d == dim else v for d, v in enumerate(self.own)
        )
        return (x * 2 + (self.core if core is None else core), z * SIDE + y)

    def at(self, dim, step):
        return lax.rem(self.own[dim] + step, SIDE)


def pick(fixed):
    return tuple(fixed.get(d, ALL) for d in range(3))


def routing_info(place, tok, ids, router_t):
    logits = nt_dot(tok, router_t)
    experts = logits.shape[1]
    small = lax.broadcasted_iota(jnp.int32, logits.shape, 1)
    id0, id1 = ids[:, 0:1], ids[:, 1:2]
    chosen = [jnp.sum(jnp.where(small == i, logits, 0.0), axis=1, keepdims=True) for i in (id0, id1)]
    first = 1.0 / (1.0 + jnp.exp(-(chosen[0] - chosen[1])))
    rows = tok.shape[0]
    lane = lax.broadcasted_iota(jnp.int32, (rows, INFO), 1)
    section, of = lane // experts, lane % experts
    is0, is1 = of == id0, of == id1
    gate = jnp.where(is0, first, jnp.where(is1, 1.0 - first, 0.0))
    named = jnp.where(is0 | is1, 1.0, 0.0)
    lower = lax.broadcasted_iota(jnp.int32, (rows, rows), 0) > lax.broadcasted_iota(
        jnp.int32, (rows, rows), 1
    )
    before = dot(jnp.where(lower, 1.0, 0.0).astype(BF16), named.astype(BF16))
    top = gate.astype(BF16).astype(F32)
    middle = (gate - top).astype(BF16).astype(F32)
    low = gate - top - middle
    info = jnp.where(section == 0, top, jnp.where(section == 1, middle, low))
    info = jnp.where(section == 3, named * (before + 1.0), info)
    return jnp.where(section > 3, 0.0, info)


def layer_kernel(
    tok_ref, router_ref, ids_ref, gate_hbm, up_hbm, down_hbm, out_ref,
    wgu, wd, mine, other, rows, scale, place_t, hidden, keep, give, got,
    relay1, final1, relay2, final2, last, w_sems, send_sems, recv_sems,
):
    place = Place()
    experts = router_ref.shape[0]
    ff_tiles = wgu.shape[0]
    width = TILE // 2

    loads = []
    for j in range(ff_tiles):
        span = pl.ds(j * width, width)
        loads.append((gate_hbm.at[0, :, span], wgu.at[j, :, pl.ds(0, width)]))
        loads.append((up_hbm.at[0, :, span], wgu.at[j, :, pl.ds(width, width)]))
    loads.append((down_hbm.at[0], wd))
    loads = [pltpu.make_async_copy(s, d, w_sems.at[i]) for i, (s, d) in enumerate(loads)]
    for copy in loads:
        copy.start()

    barrier = pltpu.get_barrier_semaphore()
    partners = [place.device(d, step) for d in range(3) for step in (1, 2, 3)]
    partners.append(place.device(core=1 - place.core))
    for partner in partners:
        pl.semaphore_signal(barrier, inc=1, device_id=partner, device_id_type=MESH)

    tok = tok_ref[...]
    block = jnp.concatenate([tok[:, :HALF].astype(F32), tok[:, HALF:].astype(F32)], axis=0)
    info = routing_info(place, tok, ids_ref[...], router_ref[...])
    mine[(*place.own, ALL, pl.ds(0, HALF))] = block.astype(BF16)
    mine[(*place.own, ALL, pl.ds(HALF, INFO))] = jnp.concatenate([info, info], axis=0).astype(BF16)
    pl.semaphore_wait(barrier, len(partners))

    started = []

    def send(src, dst, device):
        n = len(started)
        copy = pltpu.make_async_remote_copy(
            src_ref=src, dst_ref=dst, send_sem=send_sems.at[n], recv_sem=recv_sems.at[n],
            device_id=device, device_id_type=MESH,
        )
        copy.start()
        started.append(copy)
        return copy

    def block_slice(ref, part, fixed):
        return ref.at[(*pick(fixed), ALL, pl.ds(*GATHER_PARTS[part]))]

    def spread(part, fixed, dim):
        cut = ORDERS[part][0]
        half = [{**fixed, cut: pl.ds(0, 2)}, {**fixed, cut: pl.ds(2, 2)}]
        sent = {}
        for h, step in ((0, 1), (1, 3), (1, 1), (0, 3)):
            piece = block_slice(mine, part, {**half[h], dim: place.own[dim]})
            sent[h, step] = send(piece, piece, place.device(dim, step))
        return half, sent

    def relay(part, dim, half, sent):
        far = []
        for h, step in ((0, 1), (1, 3)):
            sent[h, step].wait_recv()
            piece = block_slice(mine, part, {**half[h], dim: place.at(dim, 4 - step)})
            far.append(send(piece, piece, place.device(dim, step)))
        return far

    partner = place.device(core=1 - place.core)

    def to_partner(part, fixed):
        return send(block_slice(mine, part, fixed), block_slice(other, part, fixed), partner)

    parts = range(3)
    first = []
    for part in parts:
        d1, d2, d3 = ORDERS[part]
        piece = block_slice(mine, part, dict(enumerate(place.own)))
        first.append([send(piece, piece, place.device(d1, step)) for step in (1, 2, 3)])
    second = []
    for part in parts:
        d1, d2, d3 = ORDERS[part]
        for copy in first[part]:
            copy.wait_recv()
        second.append(spread(part, {d3: place.own[d3]}, d2))
    far2 = [relay(part, ORDERS[part][1], *second[part]) for part in parts]
    third, across = [], []
    for part in parts:
        d1, d2, d3 = ORDERS[part]
        second[part][1][1, 1].wait_recv()
        second[part][1][0, 3].wait_recv()
        for copy in far2[part]:
            copy.wait_recv()
        third.append(spread(part, {}, d3))
        across.append(to_partner(part, {d3: place.own[d3]}))
    far3 = [relay(part, ORDERS[part][2], *third[part]) for part in parts]
    for part in parts:
        d3 = ORDERS[part][2]
        third[part][1][1, 1].wait_recv()
        across.append(to_partner(part, {d3: place.at(d3, 3)}))
        third[part][1][0, 3].wait_recv()
        across.append(to_partner(part, {d3: place.at(d3, 1)}))
    for part in parts:
        d3 = ORDERS[part][2]
        half = third[part][0]
        for h, copy in enumerate(far3[part]):
            copy.wait_recv()
            across.append(to_partner(part, {**half[h], d3: place.at(d3, 2)}))

    r_i = lax.broadcasted_iota(jnp.int32, (128, 256), 0)
    c_i = lax.broadcasted_iota(jnp.int32, (128, 256), 1)
    fits = (c_i // 16 == (r_i % 64) // 4) & ((c_i // 8) % 2 == r_i // 64)
    want = jnp.where(fits, r_i % 4 + 1, -1).astype(F32)
    c_t = lax.broadcasted_iota(jnp.int32, (256, 128), 0)
    r_t = lax.broadcasted_iota(jnp.int32, (256, 128), 1)
    fits_t = (c_t // 16 == (r_t % 64) // 4) & ((c_t // 8) % 2 == r_t // 64)
    want_t = jnp.where(fits_t, r_t % 4 + 1, -1).astype(F32)
    lane8 = lax.broadcasted_iota(jnp.int32, (8, INFO), 1)
    slot_lane = jnp.where(lane8 == 3 * experts + place.expert, 1.0, 0.0).astype(BF16)
    lane_t = lax.broadcasted_iota(jnp.int32, (256, INFO), 1)
    lane64 = lax.broadcasted_iota(jnp.int32, (64, INFO), 1)
    gate_lane = (lane64 % experts == place.expert) & (lane64 < 3 * experts)

    def select(source, base):
        def body(x, carry):
            g = base + x
            info = source[x, :, :, :, pl.ds(HALF, INFO)].reshape(256, INFO)
            code = nt_dot(slot_lane, info)[0:1]
            take = jnp.where(code == want, 1.0, 0.0).astype(BF16)
            code_t = jnp.sum(
                jnp.where(lane_t == 3 * experts + place.expert, info.astype(F32), 0.0),
                axis=1, keepdims=True,
            )
            place_t[g] = jnp.where(code_t == want_t, 1.0, 0.0).astype(BF16)
            gates = jnp.where(gate_lane, dot(take[0:64], info), 0.0)
            scale[g] = jnp.broadcast_to(jnp.sum(gates, axis=1, keepdims=True), (64, width))
            for n in range(0, HALF, 512):
                data = source[x, :, :, :, pl.ds(n, 512)].reshape(256, 512)
                rows[g, :, :, pl.ds(n, 512)] = dot(take, data).astype(BF16).reshape(2, 64, 512)
            return carry

        lax.fori_loop(0, SIDE, body, 0)

    select(mine, 0)
    for copy in across:
        copy.wait_recv()
    select(other, SIDE)

    for copy in loads:
        copy.wait()

    def up_body(j, carry):
        acc = dot(rows[:, 0].reshape(512, HALF), wgu[j, pl.ds(0, HALF), :])
        acc = acc + dot(rows[:, 1].reshape(512, HALF), wgu[j, pl.ds(HALF, HALF), :])
        v, u = acc[:, :width], acc[:, width:]
        act = v / (1.0 + jnp.exp(-v)) * u * scale[...].reshape(512, width)
        hidden[:, pl.ds(pl.multiple_of(j * width, width), width)] = act.astype(BF16)
        return carry

    lax.fori_loop(0, ff_tiles, up_body, 0)

    def project(part):
        start, size = SUM_PARTS[part]
        tiles = size // TILE

        def body(i, carry):
            h, col = i // tiles, pl.multiple_of(start + (i % tiles) * TILE, TILE)
            w = wd[:, pl.ds(pl.multiple_of(h * HALF + col, TILE), TILE)]
            y = dot(hidden[...], w).astype(BF16)
            rows[:, h, :, pl.ds(col, TILE)] = y.reshape(8, 64, TILE)
            return carry

        lax.fori_loop(0, 2 * tiles, body, 0)

    def scatter(part, target, base):
        cols = pl.ds(*SUM_PARTS[part])

        def body(x, carry):
            g = base + x
            y = rows[g, :, :, cols].reshape(128, SUM_PARTS[part][1])
            target[x, :, :, :, cols] = dot(place_t[g], y).astype(BF16).reshape(
                SIDE, SIDE, 16, SUM_PARTS[part][1]
            )
            return carry

        lax.fori_loop(0, SIDE, body, 0)

    def sums(part, fixed):
        return (*pick(fixed), ALL, pl.ds(*SUM_PARTS[part]))

    def add(part, fixed, pieces):
        index = sums(part, fixed)
        total = keep[index].astype(F32)
        for ref, where in pieces:
            total = total + ref[where].astype(F32)
        keep[index] = total.astype(BF16)

    def merge(part):
        def body(x, carry):
            index = (x, ALL, ALL, ALL, pl.ds(*SUM_PARTS[part]))
            keep[index] = (keep[index].astype(F32) + got[index].astype(F32)).astype(BF16)
            return carry

        lax.fori_loop(0, SIDE, body, 0)

    def open_ring(part, dim, cut, fixed, relays, finals):
        half = [{**fixed, cut: pl.ds(0, 2)}, {**fixed, cut: pl.ds(2, 2)}]
        axis = [d for d in range(3) if d not in fixed and d != dim].index(cut)

        def into(ref, way, h):
            index = [ALL] * (len(ref.shape) - 1)
            index[axis] = pl.ds(2 * h, 2)
            return ref.at[(way, *index)]

        sent = {"relay": [], "final": []}
        for h, step in ((0, 1), (1, 3)):
            src = keep.at[sums(part, {**half[h], dim: place.at(dim, 2)})]
            sent["relay"].append(send(src, relays.at[h], place.device(dim, step)))
        for way, h, step in ((0, 1, 1), (1, 0, 3)):
            src = keep.at[sums(part, {**half[h], dim: place.at(dim, step)})]
            sent["final"].append(send(src, into(finals, way, h), place.device(dim, step)))
        return half, into, sent

    def pass_ring(part, dim, relays, finals, half, into, sent):
        for h, step in ((0, 1), (1, 3)):
            sent["relay"][h].wait_recv()
            fixed = {**half[h], dim: place.at(dim, step)}
            add(part, fixed, [(relays, (h,))])
            src = keep.at[sums(part, fixed)]
            sent["final"].append(send(src, into(finals, h, h), place.device(dim, step)))

    def close_ring(part, dim, fixed, finals, sent):
        for copy in sent["final"]:
            copy.wait_recv()
        add(part, {**fixed, dim: place.own[dim]}, [(finals, (0,)), (finals, (1,))])

    rings = {}

    def begin(part):
        across_sum[part].wait_recv()
        merge(part)
        f1, f2, f3 = ORDERS[part]
        rings[part] = open_ring(part, f1, f2, {}, relay1[part], final1[part])

    across_sum = []
    for part in parts:
        project(part)
        scatter(part, give, SIDE)
        cols = pl.ds(*SUM_PARTS[part])
        across_sum.append(
            send(give.at[ALL, ALL, ALL, ALL, cols], got.at[ALL, ALL, ALL, ALL, cols], partner)
        )
        scatter(part, keep, 0)
        if part:
            begin(part - 1)
    begin(2)
    for part in parts:
        pass_ring(part, ORDERS[part][0], relay1[part], final1[part], *rings[part])
    for part in parts:
        f1, f2, f3 = ORDERS[part]
        close_ring(part, f1, {}, final1[part], rings[part][2])
        rings[part] = open_ring(part, f2, f3, {f1: place.own[f1]}, relay2[part], final2[part])
    for part in parts:
        pass_ring(part, ORDERS[part][1], relay2[part], final2[part], *rings[part])
    ends = []
    for part in parts:
        f1, f2, f3 = ORDERS[part]
        close_ring(part, f2, {f1: place.own[f1]}, final2[part], rings[part][2])
        ends.append([])
        for step in (1, 2, 3):
            where = {f1: place.own[f1], f2: place.own[f2], f3: place.at(f3, step)}
            ends[part].append(
                send(keep.at[sums(part, where)], last[part].at[step - 1], place.device(f3, step))
            )
    for part in parts:
        for copy in ends[part]:
            copy.wait_recv()
        start, size = SUM_PARTS[part]
        total = keep[sums(part, dict(enumerate(place.own)))].astype(F32)
        for k in range(3):
            total = total + last[part][k].astype(F32)
        out_ref[:, pl.ds(start, size)] = total[0:8].astype(BF16)
        out_ref[:, pl.ds(HALF + start, size)] = total[8:16].astype(BF16)

    for copy in started:
        copy.wait_send()


def ring_buffers():
    relay1, final1, relay2, final2, last = [], [], [], [], []
    for part, (start, size) in enumerate(SUM_PARTS):
        f1, f2, f3 = ORDERS[part]
        left = [d for d in range(3) if d != f1]
        relay1.append(pltpu.VMEM((2, *(2 if d == f2 else SIDE for d in left), 16, size), BF16))
        final1.append(pltpu.VMEM((2, SIDE, SIDE, 16, size), BF16))
        relay2.append(pltpu.VMEM((2, 2, 16, size), BF16))
        final2.append(pltpu.VMEM((2, SIDE, 16, size), BF16))
        last.append(pltpu.VMEM((3, 16, size), BF16))
    return relay1, final1, relay2, final2, last


COPIES = 108


def layer(tokens, router, expert_ids, w_gate, w_up, w_down):
    depth, ff = w_gate.shape[1], w_gate.shape[2]
    blocks = (SIDE, SIDE, SIDE, 16)
    vmem, anywhere = pl.BlockSpec(memory_space=pltpu.VMEM), pl.BlockSpec(memory_space=pl.ANY)
    return pl.pallas_call(
        layer_kernel,
        out_shape=jax.ShapeDtypeStruct(tokens.shape, BF16),
        in_specs=[vmem, vmem, vmem, anywhere, anywhere, anywhere],
        out_specs=vmem,
        scratch_shapes=[
            pltpu.VMEM((ff // (TILE // 2), depth, TILE), BF16),
            pltpu.VMEM((ff, depth), BF16),
            pltpu.VMEM((*blocks, HALF + INFO), BF16),
            pltpu.VMEM((*blocks, HALF + INFO), BF16),
            pltpu.VMEM((8, 2, 64, HALF), BF16),
            pltpu.VMEM((8, 64, TILE // 2), F32),
            pltpu.VMEM((8, 256, 128), BF16),
            pltpu.VMEM((512, ff), BF16),
            pltpu.VMEM((*blocks, HALF), BF16),
            pltpu.VMEM((*blocks, HALF), BF16),
            pltpu.VMEM((*blocks, HALF), BF16),
            *ring_buffers(),
            pltpu.SemaphoreType.DMA((2 * (ff // (TILE // 2)) + 1,)),
            pltpu.SemaphoreType.DMA((COPIES,)),
            pltpu.SemaphoreType.DMA((COPIES,)),
        ],
        compiler_params=pltpu.CompilerParams(
            collective_id=0, has_side_effects=True, vmem_limit_bytes=67043328
        ),
    )(tokens, router.T, expert_ids, w_gate, w_up, w_down)


def solution(mesh):
    placed = (
        P(("expert", "shard"), None),
        P(),
        P(("expert", "shard"), None),
        P("expert", None, "shard"),
        P("expert", None, "shard"),
        P("expert", "shard", None),
    )
    return jax.shard_map(
        layer, mesh=mesh, in_specs=placed, out_specs=P(("expert", "shard"), None), check_vma=False
    )
```

time: 179 us -> 91.6 us (0.51)
  Pallas kernels: 0 us -> 88.6 us
  blocking collectives: 67.8 us -> 0 us
  waiting for transfers between devices: 59.5 us -> 0 us
  matrix products: 27.9 us -> 0 us
  between operations: 13.4 us -> 0.01 us
  starting transfers between devices: 4.26 us -> 0 us
  other arithmetic: 3.13 us -> 0 us
    pallas_call x0 -> x1, Pallas kernels: none -> 88.6 us  [layer(): pl.pallas_call(layer_kernel, out_shape=jax.ShapeDtypeStruct(tokens.shape,...]
    all_to_all x2 -> x0, blocking collectives: 67.8 us -> none  [the longest x1 56.1 us: sum_at_owner(): blocks = lax.all_to_all(split_up(x, dim, devices), axis, 0, 0, tiled=True)]
    all_gather x1 -> x0, waiting for transfers between devices: 52.2 us -> none  [shards(): rows = lax.all_gather(arrived, 'shard', tiled=True)]
    dot_general x5 -> x0, matrix products: 27.9 us -> none  [the longest x1 16.4 us: shards(): jnp.dot(hidden, w_down[0], preferred_element_type=jnp.float32)]
    all_to_all x1 -> x0, waiting for transfers between devices: 7.33 us -> none  [shards(): lax.all_to_all(finished, 'expert', split_axis=0, concat_axis=0, tiled=True)]
    all_to_all x1 -> x0, starting transfers between devices: 4.25 us -> none  [shards(): lax.all_to_all(finished, 'expert', split_axis=0, concat_axis=0, tiled=True)]
    reduce_sum x1 -> x0, other arithmetic: 3.02 us -> none  [sum_at_owner(): return jnp.sum(blocks.astype(jnp.float32), axis=0)]
    unnamed x4 -> x2, local copies, waits for them, and re-layouts: 0.01 us -> 2.82 us
  transfers between devices with their start and end apart: 2 -> 0, of which waited for: 2 -> 0; matrix products, arithmetic and copies ran while one was open for 0% -> 0% of each run, Pallas kernels for 0% -> 0%
where the time goes in v2:
time: 91.6 us; the launch traced here: 91.4 us
  Pallas kernels  88.6 us (97%)
  local copies, waits for them, and re-layouts  2.82 us (3%)
    pallas_call x1, Pallas kernels, layer(): pl.pallas_call(layer_kernel, out_shape=jax.ShapeDtypeStruct(tokens.shape,...  88.6 us
    unnamed x2, local copies, waits for them, and re-layouts  2.82 us

profile of v2, /device:TPU:0, one launch (start us, length us, event | category | flops | bytes accessed | tf_op | source)
XLA Modules:
  0.0 91.4 jit_solution(5813470550810531077)
XLA Ops:
  0.0 1.3 %copy.7.ids_ref = s32[8,2]{1,0:T(8,128)} copy(s32[8,2]{0,1:T(2,128)} %param.8) | data formatting | bytes 128 | tf_op args[2]
  1.3 88.6 %shard_map.64 = bf16[8,4096]{1,0:T(8,128)(2,1)} custom-call(bf16[8,4096]{1,0:T(8,128)(2,1)} %tok_ref.1, bf16[8,4096]{1,0:T(8,128)(2,1)} %bitcast.1, s32[8,2]{1,0:T(8,128)} %copy.7.ids_ref, bf16[1,4096,896]{2,1,0:T(8,128)(2,1)} %gate_hbm.1, bf16[1,4096,896]{2,1,0:T(8,128)(2,1)} %up_hbm.1, bf16[1,896,4096]{2,1,0:T(8,128)(2,1)} %down_hbm.1), custom_call_target="tpu_custom_call" | custom-call | tf_op jit(solution)/shard_map/pallas_call | solution.py:382
  89.9 1.5 %copy.9 = bf16[8,4096]{1,0:T(8,128)(2,1)} copy(bf16[8,4096]{1,0:T(8,128)(2,1)} %shard_map.64) | data formatting | bytes 131072

commit v3 on v1

v3 whole, which is shorter than its diff:
```python
import functools

import jax
import jax.numpy as jnp
from jax import lax
from jax.experimental import pallas as pl
from jax.experimental.pallas import tpu as pltpu
from jax.sharding import PartitionSpec as P

MESH = pl.DeviceIdType.MESH
BF16, F32 = jnp.bfloat16, jnp.float32
ALL = slice(None)
FIRST, SECOND = ((0, 1), (1, 3)), ((1, 1), (0, 3))

SIDE = 4
HALF = 2048
INFO = 128
DATA = ((0, 0, 768), (768 + INFO, 768, 768), (1536 + INFO, 1536, 512))
ROUTING = 768
GATHER = (
    ((0, 256), (256, 256), (512, 256 + INFO)),
    ((896, 256), (1152, 256), (1408, 256)),
    ((1664, 256), (1920, 256)),
)
ORDERS = ((0, 1, 2), (1, 2, 0), (2, 0, 1))
TILE = 256
CHUNKS = HALF // TILE
DIRECT = 5
GATHER_SEMS, SUM_SEMS = 13, 6


def nt_dot(a, b):
    return lax.dot_general(a, b, (((1,), (1,)), ((), ())), preferred_element_type=F32)


def dot(a, b):
    return jnp.dot(a, b, preferred_element_type=F32)


class Place:
    def __init__(self):
        expert, shard = lax.axis_index("expert"), lax.axis_index("shard")
        self.expert = expert
        self.core = expert % 2
        self.own = (expert // 2, shard // SIDE, shard % SIDE)

    def device(self, dim=None, step=0, core=None):
        x, z, y = (
            lax.rem(v + step, SIDE) if d == dim else v for d, v in enumerate(self.own)
        )
        return (x * 2 + (self.core if core is None else core), z * SIDE + y)

    def at(self, dim, step):
        return lax.rem(self.own[dim] + step, SIDE)


def pick(fixed):
    return tuple(fixed.get(d, ALL) for d in range(3))


def routing_info(place, tok, ids, router_t):
    logits = nt_dot(tok, router_t)
    experts = logits.shape[1]
    small = lax.broadcasted_iota(jnp.int32, logits.shape, 1)
    same = small == lax.broadcasted_iota(jnp.int32, logits.shape, 0)
    id0, id1 = [
        jnp.sum(jnp.where(same, ids[k : k + 1, :], 0), axis=1, keepdims=True) for k in range(2)
    ]
    chosen = [jnp.sum(jnp.where(small == i, logits, 0.0), axis=1, keepdims=True) for i in (id0, id1)]
    first = 1.0 / (1.0 + jnp.exp(-(chosen[0] - chosen[1])))
    rows = tok.shape[0]
    lane = lax.broadcasted_iota(jnp.int32, (rows, INFO), 1)
    section, of = lane // experts, lane % experts
    is0, is1 = of == id0, of == id1
    gate = jnp.where(is0, first, jnp.where(is1, 1.0 - first, 0.0))
    named = jnp.where(is0 | is1, 1.0, 0.0)
    lower = lax.broadcasted_iota(jnp.int32, (rows, rows), 0) > lax.broadcasted_iota(
        jnp.int32, (rows, rows), 1
    )
    before = dot(jnp.where(lower, 1.0, 0.0).astype(BF16), named.astype(BF16))
    top = gate.astype(BF16).astype(F32)
    middle = (gate - top).astype(BF16).astype(F32)
    low = gate - top - middle
    info = jnp.where(section == 0, top, jnp.where(section == 1, middle, low))
    info = jnp.where(section == 3, named * (before + 1.0), info)
    return jnp.where(section > 3, 0.0, info)


def layer_kernel(
    tok_ref, router_ref, ids_ref, gate_hbm, up_hbm, down_hbm, out_ref,
    wgu, wd, mine, other, rows, scale, place_t, sums_gu, hidden, keep, give, got,
    relay1, final1, relay2, final2, last, w_sems, send_sems, recv_sems,
):
    place = Place()
    experts = router_ref.shape[0]
    ff_tiles = wgu.shape[0]
    width = TILE // 2

    loads = []
    for j in range(ff_tiles):
        span = pl.ds(j * width, width)
        loads.append((gate_hbm.at[0, :, span], wgu.at[j, :, pl.ds(0, width)]))
        loads.append((up_hbm.at[0, :, span], wgu.at[j, :, pl.ds(width, width)]))
    loads.append((down_hbm.at[0], wd))
    loads = [pltpu.make_async_copy(s, d, w_sems.at[i]) for i, (s, d) in enumerate(loads)]
    for copy in loads:
        copy.start()

    barrier = pltpu.get_barrier_semaphore()
    partners = [place.device(d, step) for d in range(3) for step in (1, 2, 3)]
    partners.append(place.device(core=1 - place.core))
    for partner in partners:
        pl.semaphore_signal(barrier, inc=1, device_id=partner, device_id_type=MESH)

    tok = tok_ref[...]
    block = jnp.concatenate([tok[:, :HALF].astype(F32), tok[:, HALF:].astype(F32)], axis=0)
    info = routing_info(place, tok, ids_ref[...], router_ref[...])
    block = block.astype(BF16)
    for start, first_col, size in DATA:
        mine[(*place.own, ALL, pl.ds(start, size))] = block[:, first_col : first_col + size]
    mine[(*place.own, ALL, pl.ds(ROUTING, INFO))] = jnp.concatenate([info, info], axis=0).astype(BF16)
    pl.semaphore_wait(barrier, len(partners))

    def send(src, dst, device, kind, arrival):
        pltpu.make_async_remote_copy(
            src_ref=src, dst_ref=dst, send_sem=send_sems.at[kind], recv_sem=recv_sems.at[arrival],
            device_id=device, device_id_type=MESH,
        ).start()

    def waiting(ref, kind, arrival):
        return pltpu.make_async_remote_copy(
            src_ref=ref, dst_ref=ref, send_sem=send_sems.at[kind], recv_sem=recv_sems.at[arrival],
            device_id=partner, device_id_type=MESH,
        )

    def arrive(ref, arrival):
        waiting(ref, 0, arrival).wait_recv()

    partner = place.device(core=1 - place.core)

    def block_slice(ref, chunk, part, fixed):
        return ref.at[(*pick(fixed), ALL, pl.ds(*GATHER[chunk][part]))]

    class Gather:
        def __init__(self, chunk):
            self.chunk, self.parts = chunk, range(len(GATHER[chunk]))
            self.base = chunk * GATHER_SEMS
            start = GATHER[chunk][0][0]
            self.cols = pl.ds(start, sum(size for _, size in GATHER[chunk]))
            for part in self.parts:
                piece = block_slice(mine, chunk, part, dict(enumerate(place.own)))
                for step in (1, 2, 3):
                    send(piece, piece, place.device(ORDERS[part][0], step), 0, self.base)

        def whole(self, fixed):
            return mine.at[(*pick(fixed), ALL, self.cols)]

        def pieces(self, part, fixed, dim, offset, ways, kind, arrival):
            for h, step in ways:
                where = {**fixed, ORDERS[part][0]: pl.ds(2 * h, 2), dim: place.at(dim, offset(step))}
                piece = block_slice(mine, self.chunk, part, where)
                send(piece, piece, place.device(dim, step), kind, arrival)

        def level(self, part, deep):
            d1, d2, d3 = ORDERS[part]
            return ({}, d3, 2) if deep else ({d3: place.own[d3]}, d2, 1)

        def spread(self, part, deep, ways, arrival):
            fixed, dim, kind = self.level(part, deep)
            self.pieces(part, fixed, dim, lambda step: 0, ways, kind, self.base + arrival)

        def relay(self, deep, ready, arrival):
            for part in self.parts:
                fixed, dim, kind = self.level(part, deep)
                size = block_slice(mine, self.chunk, part, {**fixed, dim: place.own[dim]})
                arrive(size, self.base + ready + part)
                self.pieces(
                    part, fixed, dim, lambda step: 4 - step, FIRST, kind, self.base + arrival(part)
                )

        def to_partner(self, step):
            for part in self.parts:
                dim = ORDERS[part][2]
                where = {dim: place.at(dim, step)}
                src = block_slice(mine, self.chunk, part, where)
                dst = block_slice(other, self.chunk, part, where)
                send(src, dst, partner, 3, self.base + 12)

        def spread2(self):
            arrive(self.whole({0: pl.ds(0, 3), 1: 0, 2: 0}), self.base)
            for part in self.parts:
                self.spread(part, False, FIRST, 1 + part)
                self.spread(part, False, SECOND, 4 + part)

        def relay2(self):
            self.relay(False, 1, lambda part: 4 + part)

        def spread3_first(self):
            for part in self.parts:
                d1, d2, d3 = ORDERS[part]
                where = {d2: pl.ds(0, 2), d3: place.own[d3]}
                arrive(block_slice(mine, self.chunk, part, where), self.base + 4 + part)
                self.spread(part, True, FIRST, 7 + part)

        def spread3_second(self):
            for part in self.parts:
                self.spread(part, True, SECOND, 10)
            self.to_partner(0)

        def relay3(self):
            self.relay(True, 7, lambda part: 11)

        def finish(self):
            arrive(self.whole({0: 0}), self.base + 10)
            self.to_partner(1)
            self.to_partner(3)
            arrive(self.whole({0: 0}), self.base + 11)
            self.to_partner(2)

        def wait_across(self):
            arrive(self.whole({}), self.base + 12)

    gathers = [Gather(chunk) for chunk in range(len(GATHER))]
    for g in gathers:
        g.spread2()
    for g in gathers:
        g.relay2()
    gathers[0].spread3_first()
    gathers[0].spread3_second()
    gathers[1].spread3_first()
    gathers[0].relay3()
    gathers[1].spread3_second()
    gathers[2].spread3_first()
    gathers[1].relay3()
    gathers[2].spread3_second()
    gathers[0].finish()

    r_i = lax.broadcasted_iota(jnp.int32, (128, 256), 0)
    c_i = lax.broadcasted_iota(jnp.int32, (128, 256), 1)
    fits = (c_i // 16 == (r_i % 64) // 4) & ((c_i // 8) % 2 == r_i // 64)
    want = jnp.where(fits, r_i % 4 + 1, -1).astype(F32)
    c_t = lax.broadcasted_iota(jnp.int32, (256, 128), 0)
    r_t = lax.broadcasted_iota(jnp.int32, (256, 128), 1)
    fits_t = (c_t // 16 == (r_t % 64) // 4) & ((c_t // 8) % 2 == r_t // 64)
    want_t = jnp.where(fits_t, r_t % 4 + 1, -1).astype(F32)
    lane8 = lax.broadcasted_iota(jnp.int32, (8, INFO), 1)
    slot_lane = jnp.where(lane8 == 3 * experts + place.expert, 1.0, 0.0).astype(BF16)
    lane_t = lax.broadcasted_iota(jnp.int32, (256, INFO), 1)
    lane64 = lax.broadcasted_iota(jnp.int32, (64, INFO), 1)
    gate_lane = (lane64 % experts == place.expert) & (lane64 < 3 * experts)

    def select(source, base, chunk):
        def body(x, carry):
            g = base + x
            info = source[x, :, :, :, pl.ds(ROUTING, INFO)].reshape(256, INFO)
            code = nt_dot(slot_lane, info)[0:1]
            take = jnp.where(code == want, 1.0, 0.0).astype(BF16)
            if chunk == 0:
                code_t = jnp.sum(
                    jnp.where(lane_t == 3 * experts + place.expert, info.astype(F32), 0.0),
                    axis=1, keepdims=True,
                )
                place_t[g] = jnp.where(code_t == want_t, 1.0, 0.0).astype(BF16)
                gates = jnp.where(gate_lane, dot(take[0:64], info), 0.0)
                scale[g] = jnp.broadcast_to(jnp.sum(gates, axis=1, keepdims=True), (64, width))
            start, first_col, size = DATA[chunk]
            data = source[x, :, :, :, pl.ds(start, size)].reshape(256, size)
            rows[g, :, :, pl.ds(first_col, size)] = dot(take, data).astype(BF16).reshape(2, 64, size)
            return carry

        lax.fori_loop(0, SIDE, body, 0)

    def products(chunk, tiles):
        start, first_col, size = DATA[chunk]
        for j in tiles:
            acc = sums_gu[j] if chunk else 0.0
            for h in range(2):
                left = rows[:, h, :, pl.ds(first_col, size)].reshape(512, size)
                acc = acc + dot(left, wgu[j, pl.ds(h * HALF + first_col, size), :])
            if chunk < len(DATA) - 1:
                sums_gu[j] = acc
                continue
            v, u = acc[:, :width], acc[:, width:]
            act = v / (1.0 + jnp.exp(-v)) * u * scale[...].reshape(512, width)
            hidden[:, pl.ds(j * width, width)] = act.astype(BF16)

    select(mine, 0, 0)
    gathers[0].wait_across()
    select(other, SIDE, 0)
    gathers[2].relay3()
    for copy in loads:
        copy.wait()
    products(0, range(4))
    gathers[1].finish()
    products(0, range(4, ff_tiles))
    select(mine, 0, 1)
    gathers[2].finish()
    gathers[1].wait_across()
    select(other, SIDE, 1)
    products(1, range(ff_tiles))
    select(mine, 0, 2)
    gathers[2].wait_across()
    select(other, SIDE, 2)
    products(2, range(ff_tiles))

    def project(k):
        for h in range(2):
            y = dot(hidden[...], wd[:, pl.ds(h * HALF + k * TILE, TILE)]).astype(BF16)
            rows[:, h, :, pl.ds(k * TILE, TILE)] = y.reshape(8, 64, TILE)

    def scatter(k, target, base):
        cols = pl.ds(k * TILE, TILE)
        for x in range(SIDE):
            y = rows[base + x, :, :, cols].reshape(128, TILE)
            placed = dot(place_t[base + x], y).astype(BF16)
            target[x, :, :, :, cols] = placed.reshape(SIDE, SIDE, 16, TILE)

    def sums(part, fixed):
        return (*pick(fixed), ALL, pl.ds(part * TILE, TILE))

    def add(part, fixed, pieces):
        index = sums(part, fixed)
        total = keep[index].astype(F32)
        for ref, where in pieces:
            total = total + ref[where].astype(F32)
        keep[index] = total.astype(BF16)

    def merge(part):
        for x in range(SIDE):
            add(part, {0: x}, [(got, sums(part, {0: x}))])

    sum_base = len(GATHER) * GATHER_SEMS

    def arrival(k, what):
        return sum_base + k * SUM_SEMS + what

    def ring(k, deep):
        f1, f2, f3 = ORDERS[k % 3]
        if deep:
            return f2, f3, {f1: place.own[f1]}, relay2[k], final2[k], 6, arrival(k, 3)
        return f1, f2, {}, relay1[k], final1[k], 5, arrival(k, 1)

    def into(ref, k, dim, cut, fixed, way, h):
        axis = [d for d in range(3) if d not in fixed and d != dim].index(cut)
        index = [ALL] * (len(ref.shape) - 1)
        index[axis] = pl.ds(2 * h, 2)
        return ref.at[(way, *index)]

    def open_ring(k, deep):
        dim, cut, fixed, relays, finals, kind, base = ring(k, deep)
        for h, step in FIRST:
            src = keep.at[sums(k, {**fixed, cut: pl.ds(2 * h, 2), dim: place.at(dim, 2)})]
            send(src, relays.at[h], place.device(dim, step), kind, base)
        for way, h, step in ((0, 1, 1), (1, 0, 3)):
            src = keep.at[sums(k, {**fixed, cut: pl.ds(2 * h, 2), dim: place.at(dim, step)})]
            dst = into(finals, k, dim, cut, fixed, way, h)
            send(src, dst, place.device(dim, step), kind, base + 1)

    def pass_ring(k, deep):
        dim, cut, fixed, relays, finals, kind, base = ring(k, deep)
        arrive(relays, base)
        for h, step in FIRST:
            where = {**fixed, cut: pl.ds(2 * h, 2), dim: place.at(dim, step)}
            add(k, where, [(relays, (h,))])
            dst = into(finals, k, dim, cut, fixed, h, h)
            send(keep.at[sums(k, where)], dst, place.device(dim, step), kind, base + 1)

    def close_ring(k, deep):
        dim, cut, fixed, relays, finals, kind, base = ring(k, deep)
        arrive(finals, base + 1)
        add(k, {**fixed, dim: place.own[dim]}, [(finals, (i,)) for i in range(finals.shape[0])])

    def compute(k):
        project(k)
        scatter(k, give, SIDE)
        piece = sums(k, {})
        send(give.at[piece], got.at[piece], partner, 4, arrival(k, 0))
        scatter(k, keep, 0)

    def begin(k):
        arrive(got.at[sums(k, {})], arrival(k, 0))
        merge(k)
        open_ring(k, False)

    def pass_first(k):
        pass_ring(k, False)

    def close_first(k):
        close_ring(k, False)
        if k < DIRECT:
            open_ring(k, True)
            return
        f1, f2, f3 = ORDERS[k % 3]
        for step in (1, 3, 2):
            src = keep.at[sums(k, {f1: place.own[f1], f2: place.at(f2, step)})]
            send(src, final2[k].at[step - 1], place.device(f2, step), 6, arrival(k, 4))

    def pass_second(k):
        if k < DIRECT:
            pass_ring(k, True)

    def close_second(k):
        close_ring(k, True)
        f1, f2, f3 = ORDERS[k % 3]
        for step in (1, 3, 2):
            where = {f1: place.own[f1], f2: place.own[f2], f3: place.at(f3, step)}
            src = keep.at[sums(k, where)]
            send(src, last[k].at[step - 1], place.device(f3, step), 7, arrival(k, 5))

    def finish(k):
        arrive(last[k], arrival(k, 5))
        total = keep[sums(k, dict(enumerate(place.own)))].astype(F32)
        for i in range(3):
            total = total + last[k][i].astype(F32)
        out_ref[:, pl.ds(k * TILE, TILE)] = total[0:8].astype(BF16)
        out_ref[:, pl.ds(HALF + k * TILE, TILE)] = total[8:16].astype(BF16)

    plan = []
    for k in range(CHUNKS):
        plan.append((1.1 * k, compute, k))
        plan.append((1.1 * k + 2.25, begin, k))
        closed = 13.6 + 0.9 * k
        second = closed + (6.4 if k < DIRECT else 4.5)
        plan.append((9.3 + k, pass_first, k))
        plan.append((closed, close_first, k))
        plan.append((closed + 3.2, pass_second, k))
        plan.append((second, close_second, k))
        plan.append((second + 4.0, finish, k))
    for when, step, k in sorted(plan, key=lambda entry: entry[0]):
        step(k)

    for kind, sent in enumerate(
        (
            mine.at[pl.ds(0, 3), 0, 0], mine.at[pl.ds(0, 3), :, 0], mine.at[pl.ds(0, 3)], mine,
            keep, keep.at[pl.ds(0, 3)], keep.at[pl.ds(0, 3), :, 0], keep.at[pl.ds(0, 3), 0, 0],
        )
    ):
        waiting(sent, kind, 0).wait_send()


def ring_buffers():
    relay1, final1, relay2, final2, last = [], [], [], [], []
    for k in range(CHUNKS):
        f1, f2, f3 = ORDERS[k % 3]
        left = [d for d in range(3) if d != f1]
        relay1.append(pltpu.VMEM((2, *(2 if d == f2 else SIDE for d in left), 16, TILE), BF16))
        final1.append(pltpu.VMEM((2, SIDE, SIDE, 16, TILE), BF16))
        relay2.append(pltpu.VMEM((2, 2, 16, TILE), BF16))
        final2.append(pltpu.VMEM((2 if k < DIRECT else 3, SIDE, 16, TILE), BF16))
        last.append(pltpu.VMEM((3, 16, TILE), BF16))
    return relay1, final1, relay2, final2, last


def layer(tokens, router, expert_ids, w_gate, w_up, w_down):
    depth, ff = w_gate.shape[1], w_gate.shape[2]
    blocks = (SIDE, SIDE, SIDE, 16)
    vmem, anywhere = pl.BlockSpec(memory_space=pltpu.VMEM), pl.BlockSpec(memory_space=pl.ANY)
    return pl.pallas_call(
        layer_kernel,
        out_shape=jax.ShapeDtypeStruct(tokens.shape, BF16),
        in_specs=[vmem, vmem, vmem, anywhere, anywhere, anywhere],
        out_specs=vmem,
        scratch_shapes=[
            pltpu.VMEM((ff // (TILE // 2), depth, TILE), BF16),
            pltpu.VMEM((ff, depth), BF16),
            pltpu.VMEM((*blocks, HALF + INFO), BF16),
            pltpu.VMEM((*blocks, HALF + INFO), BF16),
            pltpu.VMEM((8, 2, 64, HALF), BF16),
            pltpu.VMEM((8, 64, TILE // 2), F32),
            pltpu.VMEM((8, 256, 128), BF16),
            pltpu.VMEM((ff // (TILE // 2), 512, TILE), F32),
            pltpu.VMEM((512, ff), BF16),
            pltpu.VMEM((*blocks, HALF), BF16),
            pltpu.VMEM((*blocks, HALF), BF16),
            pltpu.VMEM((*blocks, HALF), BF16),
            *ring_buffers(),
            pltpu.SemaphoreType.DMA((2 * (ff // (TILE // 2)) + 1,)),
            pltpu.SemaphoreType.DMA((8,)),
            pltpu.SemaphoreType.DMA((len(GATHER) * GATHER_SEMS + CHUNKS * SUM_SEMS,)),
        ],
        compiler_params=pltpu.CompilerParams(
            collective_id=0, has_side_effects=True, vmem_limit_bytes=67043328
        ),
    )(tokens, router.T, expert_ids.T, w_gate, w_up, w_down)


def solution(mesh):
    placed = (
        P(("expert", "shard"), None),
        P(),
        P(("expert", "shard"), None),
        P("expert", None, "shard"),
        P("expert", None, "shard"),
        P("expert", "shard", None),
    )
    return jax.shard_map(
        layer, mesh=mesh, in_specs=placed, out_specs=P(("expert", "shard"), None), check_vma=False
    )
```

time: 179 us -> 83.2 us (0.46)
  Pallas kernels: 0 us -> 81.5 us
  blocking collectives: 67.8 us -> 0 us
  waiting for transfers between devices: 59.5 us -> 0 us
  matrix products: 27.9 us -> 0 us
  between operations: 13.4 us -> 0.01 us
  starting transfers between devices: 4.26 us -> 0 us
  other arithmetic: 3.13 us -> 0 us
    pallas_call x0 -> x1, Pallas kernels: none -> 81.5 us  [layer(): pl.pallas_call(layer_kernel, out_shape=jax.ShapeDtypeStruct(tokens.shape,...]
    all_to_all x2 -> x0, blocking collectives: 67.8 us -> none  [the longest x1 56.1 us: sum_at_owner(): blocks = lax.all_to_all(split_up(x, dim, devices), axis, 0, 0, tiled=True)]
    all_gather x1 -> x0, waiting for transfers between devices: 52.2 us -> none  [shards(): rows = lax.all_gather(arrived, 'shard', tiled=True)]
    dot_general x5 -> x0, matrix products: 27.9 us -> none  [the longest x1 16.4 us: shards(): jnp.dot(hidden, w_down[0], preferred_element_type=jnp.float32)]
    all_to_all x1 -> x0, waiting for transfers between devices: 7.33 us -> none  [shards(): lax.all_to_all(finished, 'expert', split_axis=0, concat_axis=0, tiled=True)]
    all_to_all x1 -> x0, starting transfers between devices: 4.25 us -> none  [shards(): lax.all_to_all(finished, 'expert', split_axis=0, concat_axis=0, tiled=True)]
    reduce_sum x1 -> x0, other arithmetic: 3.02 us -> none  [sum_at_owner(): return jnp.sum(blocks.astype(jnp.float32), axis=0)]
  transfers between devices with their start and end apart: 2 -> 0, of which waited for: 2 -> 0; matrix products, arithmetic and copies ran while one was open for 0% -> 0% of each run, Pallas kernels for 0% -> 0%
where the time goes in v3:
time: 83.2 us; the launch traced here: 83 us
  Pallas kernels  81.5 us (98%)
  local copies, waits for them, and re-layouts  1.47 us (2%)
    pallas_call x1, Pallas kernels, layer(): pl.pallas_call(layer_kernel, out_shape=jax.ShapeDtypeStruct(tokens.shape,...  81.5 us

profile of v3, /device:TPU:0, one launch (start us, length us, event | category | flops | bytes accessed | tf_op | source)
XLA Modules:
  0.0 83.0 jit_solution(12174428822862813304)
XLA Ops:
  0.0 81.5 %shard_map.64 = bf16[8,4096]{1,0:T(8,128)(2,1)} custom-call(bf16[8,4096]{1,0:T(8,128)(2,1)} %tok_ref.1, bf16[8,4096]{1,0:T(8,128)(2,1)} %bitcast.2, s32[2,8]{1,0:T(2,128)} %bitcast.3, bf16[1,4096,896]{2,1,0:T(8,128)(2,1)} %gate_hbm.1, bf16[1,4096,896]{2,1,0:T(8,128)(2,1)} %up_hbm.1, bf16[1,896,4096]{2,1,0:T(8,128)(2,1)} %down_hbm.1), custom_call_target="tpu_custom_call" | custom-call | tf_op jit(solution)/shard_map/pallas_call | solution.py:458
  81.5 1.5 %copy.8 = bf16[8,4096]{1,0:T(8,128)(2,1)} copy(bf16[8,4096]{1,0:T(8,128)(2,1)} %shard_map.64) | data formatting | bytes 131072

commit v4 on v3

--- a/solution.py
+++ b/solution.py
@@ -11,6 +11,7 @@
 BF16, F32 = jnp.bfloat16, jnp.float32
 ALL = slice(None)
 FIRST, SECOND = ((0, 1), (1, 3)), ((1, 1), (0, 3))
+AROUND = (1, 3, 2)
 
 SIDE = 4
 HALF = 2048
@@ -26,7 +27,7 @@
 TILE = 256
 CHUNKS = HALF // TILE
 DIRECT = 5
-GATHER_SEMS, SUM_SEMS = 13, 6
+GATHER_SEMS, SUM_SEMS = 16, 6
 
 
 def nt_dot(a, b):
@@ -88,7 +89,7 @@
 
 def layer_kernel(
     tok_ref, router_ref, ids_ref, gate_hbm, up_hbm, down_hbm, out_ref,
-    wgu, wd, mine, other, rows, scale, place_t, sums_gu, hidden, keep, give, got,
+    wgu, wd, mine, other, rows, scale, take, place_t, sums_gu, hidden, keep, give, got,
     relay1, final1, relay2, final2, last, w_sems, send_sems, recv_sems,
 ):
     place = Place()
@@ -161,21 +162,20 @@
                 piece = block_slice(mine, self.chunk, part, where)
                 send(piece, piece, place.device(dim, step), kind, arrival)
 
-        def level(self, part, deep):
+        def level(self, part, deep, at2):
             d1, d2, d3 = ORDERS[part]
-            return ({}, d3, 2) if deep else ({d3: place.own[d3]}, d2, 1)
-
-        def spread(self, part, deep, ways, arrival):
-            fixed, dim, kind = self.level(part, deep)
-            self.pieces(part, fixed, dim, lambda step: 0, ways, kind, self.base + arrival)
-
-        def relay(self, deep, ready, arrival):
-            for part in self.parts:
-                fixed, dim, kind = self.level(part, deep)
-                size = block_slice(mine, self.chunk, part, {**fixed, dim: place.own[dim]})
-                arrive(size, self.base + ready + part)
+            if deep:
+                return [({d2: place.at(d2, o)}, d3, 2) for o in at2]
+            return [({d3: place.own[d3]}, d2, 1)]
+
+        def spread(self, part, deep, ways, arrival, at2=()):
+            for fixed, dim, kind in self.level(part, deep, at2):
+                self.pieces(part, fixed, dim, lambda step: 0, ways, kind, self.base + arrival)
+
+        def relay(self, part, deep, arrival, at2=()):
+            for fixed, dim, kind in self.level(part, deep, at2):
                 self.pieces(
-                    part, fixed, dim, lambda step: 4 - step, FIRST, kind, self.base + arrival(part)
+                    part, fixed, dim, lambda step: 4 - step, FIRST, kind, self.base + arrival
                 )
 
         def to_partner(self, step):
@@ -192,23 +192,43 @@
                 self.spread(part, False, FIRST, 1 + part)
                 self.spread(part, False, SECOND, 4 + part)
 
+        def early3(self):
+            for part in self.parts:
+                self.spread(part, True, FIRST, 13 + part, (0,))
+                self.spread(part, True, SECOND, 10, (0,))
+
+        def four(self, part):
+            d1, d2, d3 = ORDERS[part]
+            return block_slice(mine, self.chunk, part, {d2: place.own[d2], d3: place.own[d3]})
+
         def relay2(self):
-            self.relay(False, 1, lambda part: 4 + part)
+            for part in self.parts:
+                arrive(self.four(part), self.base + 1 + part)
+                self.relay(part, False, 4 + part)
+
+        def relay3_early(self):
+            for part in self.parts:
+                arrive(self.four(part), self.base + 13 + part)
+                self.relay(part, True, 11, (0,))
 
         def spread3_first(self):
             for part in self.parts:
                 d1, d2, d3 = ORDERS[part]
                 where = {d2: pl.ds(0, 2), d3: place.own[d3]}
                 arrive(block_slice(mine, self.chunk, part, where), self.base + 4 + part)
-                self.spread(part, True, FIRST, 7 + part)
+                self.spread(part, True, FIRST, 7 + part, AROUND)
 
         def spread3_second(self):
             for part in self.parts:
-                self.spread(part, True, SECOND, 10)
+                self.spread(part, True, SECOND, 10, AROUND)
             self.to_partner(0)
 
         def relay3(self):
-            self.relay(True, 7, lambda part: 11)
+            for part in self.parts:
+                d1, d2, d3 = ORDERS[part]
+                where = {d2: pl.ds(0, 3), d3: place.own[d3]}
+                arrive(block_slice(mine, self.chunk, part, where), self.base + 7 + part)
+                self.relay(part, True, 11, AROUND)
 
         def finish(self):
             arrive(self.whole({0: 0}), self.base + 10)
@@ -224,7 +244,11 @@
     for g in gathers:
         g.spread2()
     for g in gathers:
+        g.early3()
+    for g in gathers:
         g.relay2()
+    for g in gathers:
+        g.relay3_early()
     gathers[0].spread3_first()
     gathers[0].spread3_second()
     gathers[1].spread3_first()
@@ -249,26 +273,31 @@
     lane64 = lax.broadcasted_iota(jnp.int32, (64, INFO), 1)
     gate_lane = (lane64 % experts == place.expert) & (lane64 < 3 * experts)
 
-    def select(source, base, chunk):
-        def body(x, carry):
+    def route(source, base):
+        for x in range(SIDE):
             g = base + x
             info = source[x, :, :, :, pl.ds(ROUTING, INFO)].reshape(256, INFO)
             code = nt_dot(slot_lane, info)[0:1]
-            take = jnp.where(code == want, 1.0, 0.0).astype(BF16)
-            if chunk == 0:
-                code_t = jnp.sum(
-                    jnp.where(lane_t == 3 * experts + place.expert, info.astype(F32), 0.0),
-                    axis=1, keepdims=True,
-                )
-                place_t[g] = jnp.where(code_t == want_t, 1.0, 0.0).astype(BF16)
-                gates = jnp.where(gate_lane, dot(take[0:64], info), 0.0)
-                scale[g] = jnp.broadcast_to(jnp.sum(gates, axis=1, keepdims=True), (64, width))
-            start, first_col, size = DATA[chunk]
+            take[g] = jnp.where(code == want, 1.0, 0.0).astype(BF16)
+
+    def route_back(source, base):
+        for x in range(SIDE):
+            g = base + x
+            info = source[x, :, :, :, pl.ds(ROUTING, INFO)].reshape(256, INFO)
+            code_t = jnp.sum(
+                jnp.where(lane_t == 3 * experts + place.expert, info.astype(F32), 0.0),
+                axis=1, keepdims=True,
+            )
+            place_t[g] = jnp.where(code_t == want_t, 1.0, 0.0).astype(BF16)
+            gates = jnp.where(gate_lane, dot(take[g, pl.ds(0, 64)], info), 0.0)
+            scale[g] = jnp.broadcast_to(jnp.sum(gates, axis=1, keepdims=True), (64, width))
+
+    def select(source, base, chunk):
+        start, first_col, size = DATA[chunk]
+        for x in range(SIDE):
             data = source[x, :, :, :, pl.ds(start, size)].reshape(256, size)
-            rows[g, :, :, pl.ds(first_col, size)] = dot(take, data).astype(BF16).reshape(2, 64, size)
-            return carry
-
-        lax.fori_loop(0, SIDE, body, 0)
+            chosen = dot(take[base + x], data).astype(BF16).reshape(2, 64, size)
+            rows[base + x, :, :, pl.ds(first_col, size)] = chosen
 
     def products(chunk, tiles):
         start, first_col, size = DATA[chunk]
@@ -284,21 +313,25 @@
             act = v / (1.0 + jnp.exp(-v)) * u * scale[...].reshape(512, width)
             hidden[:, pl.ds(j * width, width)] = act.astype(BF16)
 
+    gathers[2].relay3()
+    route(mine, 0)
     select(mine, 0, 0)
+    route_back(mine, 0)
     gathers[0].wait_across()
+    route(other, SIDE)
     select(other, SIDE, 0)
-    gathers[2].relay3()
     for copy in loads:
         copy.wait()
     products(0, range(4))
     gathers[1].finish()
     products(0, range(4, ff_tiles))
+    gathers[2].finish()
     select(mine, 0, 1)
-    gathers[2].finish()
+    route_back(other, SIDE)
     gathers[1].wait_across()
     select(other, SIDE, 1)
+    select(mine, 0, 2)
     products(1, range(ff_tiles))
-    select(mine, 0, 2)
     gathers[2].wait_across()
     select(other, SIDE, 2)
     products(2, range(ff_tiles))
@@ -421,7 +454,7 @@
         plan.append((1.1 * k + 2.25, begin, k))
         closed = 13.6 + 0.9 * k
         second = closed + (6.4 if k < DIRECT else 4.5)
-        plan.append((9.3 + k, pass_first, k))
+        plan.append((7.3 + k, pass_first, k))
         plan.append((closed, close_first, k))
         plan.append((closed + 3.2, pass_second, k))
         plan.append((second, close_second, k))
@@ -467,6 +500,7 @@
             pltpu.VMEM((*blocks, HALF + INFO), BF16),
             pltpu.VMEM((8, 2, 64, HALF), BF16),
             pltpu.VMEM((8, 64, TILE // 2), F32),
+            pltpu.VMEM((8, 128, 256), BF16),
             pltpu.VMEM((8, 256, 128), BF16),
             pltpu.VMEM((ff // (TILE // 2), 512, TILE), F32),
             pltpu.VMEM((512, ff), BF16),

time: 83.2 us -> 75.6 us (0.909)
  Pallas kernels: 81.5 us -> 74 us
    pallas_call x1, Pallas kernels: 81.5 us -> 74 us  [layer(): pl.pallas_call(layer_kernel, out_shape=jax.ShapeDtypeStruct(tokens.shape,...]
where the time goes in v4:
time: 75.6 us; the launch traced here: 75.4 us
  Pallas kernels  74 us (98%)
  local copies, waits for them, and re-layouts  1.47 us (2%)
    pallas_call x1, Pallas kernels, layer(): pl.pallas_call(layer_kernel, out_shape=jax.ShapeDtypeStruct(tokens.shape,...  74 us

profile of v4, /device:TPU:0, one launch (start us, length us, event | category | flops | bytes accessed | tf_op | source)
XLA Modules:
  0.0 75.4 jit_solution(10284037846490234178)
XLA Ops:
  0.0 74.0 %shard_map.64 = bf16[8,4096]{1,0:T(8,128)(2,1)} custom-call(bf16[8,4096]{1,0:T(8,128)(2,1)} %tok_ref.1, bf16[8,4096]{1,0:T(8,128)(2,1)} %bitcast.2, s32[2,8]{1,0:T(2,128)} %bitcast.3, bf16[1,4096,896]{2,1,0:T(8,128)(2,1)} %gate_hbm.1, bf16[1,4096,896]{2,1,0:T(8,128)(2,1)} %up_hbm.1, bf16[1,896,4096]{2,1,0:T(8,128)(2,1)} %down_hbm.1), custom_call_target="tpu_custom_call" | custom-call | tf_op jit(solution)/shard_map/pallas_call | solution.py:491
  74.0 1.5 %copy.8 = bf16[8,4096]{1,0:T(8,128)(2,1)} copy(bf16[8,4096]{1,0:T(8,128)(2,1)} %shard_map.64) | data formatting | bytes 131072

commit v5 on v4

--- a/solution.py
+++ b/solution.py
@@ -27,7 +27,7 @@
 TILE = 256
 CHUNKS = HALF // TILE
 DIRECT = 5
-GATHER_SEMS, SUM_SEMS = 16, 6
+GATHER_SEMS, SUM_SEMS = 16, 8
 
 
 def nt_dot(a, b):
@@ -88,14 +88,30 @@
 
 
 def layer_kernel(
-    tok_ref, router_ref, ids_ref, gate_hbm, up_hbm, down_hbm, out_ref,
+    tok_hbm, router_hbm, ids_hbm, gate_hbm, up_hbm, down_hbm, out_hbm,
+    tok_ref, router_ref, ids_ref, out_ref,
     wgu, wd, mine, other, rows, scale, take, place_t, sums_gu, hidden, keep, give, got,
-    relay1, final1, relay2, final2, last, w_sems, send_sems, recv_sems,
+    relay1, final1, relay2, final2, last, in_sems, w_sems, send_sems, recv_sems,
 ):
     place = Place()
     experts = router_ref.shape[0]
     ff_tiles = wgu.shape[0]
     width = TILE // 2
+
+    inputs = [
+        pltpu.make_async_copy(src, dst, in_sems.at[i])
+        for i, (src, dst) in enumerate(
+            ((tok_hbm, tok_ref), (ids_hbm, ids_ref), (router_hbm, router_ref))
+        )
+    ]
+    for copy in inputs:
+        copy.start()
+
+    barrier = pltpu.get_barrier_semaphore()
+    partners = [place.device(d, step) for d in range(3) for step in (1, 2, 3)]
+    partners.append(place.device(core=1 - place.core))
+    for partner in partners:
+        pl.semaphore_signal(barrier, inc=1, device_id=partner, device_id_type=MESH)
 
     loads = []
     for j in range(ff_tiles):
@@ -107,12 +123,8 @@
     for copy in loads:
         copy.start()
 
-    barrier = pltpu.get_barrier_semaphore()
-    partners = [place.device(d, step) for d in range(3) for step in (1, 2, 3)]
-    partners.append(place.device(core=1 - place.core))
-    for partner in partners:
-        pl.semaphore_signal(barrier, inc=1, device_id=partner, device_id_type=MESH)
-
+    for copy in inputs:
+        copy.wait()
     tok = tok_ref[...]
     block = jnp.concatenate([tok[:, :HALF].astype(F32), tok[:, HALF:].astype(F32)], axis=0)
     info = routing_info(place, tok, ids_ref[...], router_ref[...])
@@ -367,41 +379,65 @@
     def arrival(k, what):
         return sum_base + k * SUM_SEMS + what
 
-    def ring(k, deep):
-        f1, f2, f3 = ORDERS[k % 3]
-        if deep:
-            return f2, f3, {f1: place.own[f1]}, relay2[k], final2[k], 6, arrival(k, 3)
-        return f1, f2, {}, relay1[k], final1[k], 5, arrival(k, 1)
-
-    def into(ref, k, dim, cut, fixed, way, h):
-        axis = [d for d in range(3) if d not in fixed and d != dim].index(cut)
-        index = [ALL] * (len(ref.shape) - 1)
-        index[axis] = pl.ds(2 * h, 2)
-        return ref.at[(way, *index)]
-
-    def open_ring(k, deep):
-        dim, cut, fixed, relays, finals, kind, base = ring(k, deep)
+    def line(ref, k, at2):
+        f1, f2, f3 = ORDERS[k % 3]
+        index = [ALL] * len(ref.shape)
+        index[1 + [d for d in range(3) if d != f1].index(f2)] = at2
+        return ref.at[tuple(index)]
+
+    def into(ref, k, offset, way, h):
+        f1, f2, f3 = ORDERS[k % 3]
+        index = {f2: place.at(f2, offset)}
+        if h is not None:
+            index[f3] = pl.ds(2 * h, 2)
+        return (way, *(index.get(d, ALL) for d in range(3) if d != f1))
+
+    def half_line(k, step, offset, h):
+        f1, f2, f3 = ORDERS[k % 3]
+        return {f1: place.at(f1, step), f2: place.at(f2, offset), f3: pl.ds(2 * h, 2)}
+
+    def open_first(k, offsets, base):
+        f1 = ORDERS[k % 3][0]
+        for h, step in FIRST:
+            for offset in offsets:
+                src = keep.at[sums(k, half_line(k, 2, offset, h))]
+                dst = relay1[k].at[into(relay1[k], k, offset, h, None)]
+                send(src, dst, place.device(f1, step), 5, base)
+        for way, h, step in ((0, 1, 1), (1, 0, 3)):
+            for offset in offsets:
+                src = keep.at[sums(k, half_line(k, step, offset, h))]
+                dst = final1[k].at[into(final1[k], k, offset, way, h)]
+                send(src, dst, place.device(f1, step), 5, base + 1)
+
+    def pass_on(k, offsets, base):
+        for h, step in FIRST:
+            for offset in offsets:
+                where = half_line(k, step, offset, h)
+                add(k, where, [(relay1[k], into(relay1[k], k, offset, h, None))])
+                dst = final1[k].at[into(final1[k], k, offset, h, h)]
+                send(
+                    keep.at[sums(k, where)], dst, place.device(ORDERS[k % 3][0], step), 5, base + 1
+                )
+
+    def take_in(k, offsets):
+        f1, f2, f3 = ORDERS[k % 3]
+        for offset in offsets:
+            where = {f1: place.own[f1], f2: place.at(f2, offset)}
+            add(k, where, [(final1[k], into(final1[k], k, offset, way, None)) for way in range(2)])
+
+    def open_second(k):
+        dim, cut, fixed = second_ring(k)
         for h, step in FIRST:
             src = keep.at[sums(k, {**fixed, cut: pl.ds(2 * h, 2), dim: place.at(dim, 2)})]
-            send(src, relays.at[h], place.device(dim, step), kind, base)
+            send(src, relay2[k].at[h], place.device(dim, step), 6, arrival(k, 3))
         for way, h, step in ((0, 1, 1), (1, 0, 3)):
             src = keep.at[sums(k, {**fixed, cut: pl.ds(2 * h, 2), dim: place.at(dim, step)})]
-            dst = into(finals, k, dim, cut, fixed, way, h)
-            send(src, dst, place.device(dim, step), kind, base + 1)
-
-    def pass_ring(k, deep):
-        dim, cut, fixed, relays, finals, kind, base = ring(k, deep)
-        arrive(relays, base)
-        for h, step in FIRST:
-            where = {**fixed, cut: pl.ds(2 * h, 2), dim: place.at(dim, step)}
-            add(k, where, [(relays, (h,))])
-            dst = into(finals, k, dim, cut, fixed, h, h)
-            send(keep.at[sums(k, where)], dst, place.device(dim, step), kind, base + 1)
-
-    def close_ring(k, deep):
-        dim, cut, fixed, relays, finals, kind, base = ring(k, deep)
-        arrive(finals, base + 1)
-        add(k, {**fixed, dim: place.own[dim]}, [(finals, (i,)) for i in range(finals.shape[0])])
+            dst = final2[k].at[way, pl.ds(2 * h, 2)]
+            send(src, dst, place.device(dim, step), 6, arrival(k, 4))
+
+    def second_ring(k):
+        f1, f2, f3 = ORDERS[k % 3]
+        return f2, f3, {f1: place.own[f1]}
 
     def compute(k):
         project(k)
@@ -413,27 +449,50 @@
     def begin(k):
         arrive(got.at[sums(k, {})], arrival(k, 0))
         merge(k)
-        open_ring(k, False)
+        open_first(k, AROUND, arrival(k, 1))
 
     def pass_first(k):
-        pass_ring(k, False)
+        arrive(line(relay1[k], k, pl.ds(0, 3)), arrival(k, 1))
+        pass_on(k, AROUND, arrival(k, 1))
 
     def close_first(k):
-        close_ring(k, False)
+        arrive(line(final1[k], k, pl.ds(0, 3)), arrival(k, 2))
+        take_in(k, AROUND)
         if k < DIRECT:
-            open_ring(k, True)
+            open_second(k)
             return
         f1, f2, f3 = ORDERS[k % 3]
         for step in (1, 3, 2):
             src = keep.at[sums(k, {f1: place.own[f1], f2: place.at(f2, step)})]
             send(src, final2[k].at[step - 1], place.device(f2, step), 6, arrival(k, 4))
 
+    def open_late(k):
+        open_first(k, (0,), arrival(k, 6))
+
+    def pass_late(k):
+        arrive(line(relay1[k], k, 0), arrival(k, 6))
+        pass_on(k, (0,), arrival(k, 6))
+
+    def close_late(k):
+        arrive(line(final1[k], k, 0), arrival(k, 7))
+        take_in(k, (0,))
+
     def pass_second(k):
-        if k < DIRECT:
-            pass_ring(k, True)
+        if k >= DIRECT:
+            return
+        dim, cut, fixed = second_ring(k)
+        arrive(relay2[k], arrival(k, 3))
+        for h, step in FIRST:
+            where = {**fixed, cut: pl.ds(2 * h, 2), dim: place.at(dim, step)}
+            add(k, where, [(relay2[k], (h,))])
+            dst = final2[k].at[h, pl.ds(2 * h, 2)]
+            send(keep.at[sums(k, where)], dst, place.device(dim, step), 6, arrival(k, 4))
 
     def close_second(k):
-        close_ring(k, True)
+        arrive(final2[k], arrival(k, 4))
+        f1, f2, f3 = ORDERS[k % 3]
+        ways = range(final2[k].shape[0])
+        add(k, {f1: place.own[f1], f2: place.own[f2]}, [(final2[k], (i,)) for i in ways])
         f1, f2, f3 = ORDERS[k % 3]
         for step in (1, 3, 2):
             where = {f1: place.own[f1], f2: place.own[f2], f3: place.at(f3, step)}
@@ -447,20 +506,28 @@
             total = total + last[k][i].astype(F32)
         out_ref[:, pl.ds(k * TILE, TILE)] = total[0:8].astype(BF16)
         out_ref[:, pl.ds(HALF + k * TILE, TILE)] = total[8:16].astype(BF16)
+        for h in range(2):
+            cols = pl.ds(h * HALF + k * TILE, TILE)
+            pltpu.make_async_copy(out_ref.at[:, cols], out_hbm.at[:, cols], in_sems.at[3]).start()
 
     plan = []
     for k in range(CHUNKS):
         plan.append((1.1 * k, compute, k))
         plan.append((1.1 * k + 2.25, begin, k))
-        closed = 13.6 + 0.9 * k
-        second = closed + (6.4 if k < DIRECT else 4.5)
-        plan.append((7.3 + k, pass_first, k))
+        closed = 11.8 + 0.85 * k
+        second = max(closed + (6.2 if k < DIRECT else 4.2), 19.3 + 0.45 * k)
+        plan.append((7.3 + 0.9 * k, pass_first, k))
         plan.append((closed, close_first, k))
-        plan.append((closed + 3.2, pass_second, k))
+        plan.append((closed + 3.1, pass_second, k))
+        plan.append((11.0 + 0.5 * k, open_late, k))
+        plan.append((15.5 + 0.5 * k, pass_late, k))
+        plan.append((19.0 + 0.45 * k, close_late, k))
         plan.append((second, close_second, k))
         plan.append((second + 4.0, finish, k))
     for when, step, k in sorted(plan, key=lambda entry: entry[0]):
         step(k)
+
+    pltpu.make_async_copy(out_ref, out_hbm, in_sems.at[3]).wait()
 
     for kind, sent in enumerate(
         (
@@ -476,7 +543,7 @@
     for k in range(CHUNKS):
         f1, f2, f3 = ORDERS[k % 3]
         left = [d for d in range(3) if d != f1]
-        relay1.append(pltpu.VMEM((2, *(2 if d == f2 else SIDE for d in left), 16, TILE), BF16))
+        relay1.append(pltpu.VMEM((2, *(2 if d == f3 else SIDE for d in left), 16, TILE), BF16))
         final1.append(pltpu.VMEM((2, SIDE, SIDE, 16, TILE), BF16))
         relay2.append(pltpu.VMEM((2, 2, 16, TILE), BF16))
         final2.append(pltpu.VMEM((2 if k < DIRECT else 3, SIDE, 16, TILE), BF16))
@@ -487,13 +554,17 @@
 def layer(tokens, router, expert_ids, w_gate, w_up, w_down):
     depth, ff = w_gate.shape[1], w_gate.shape[2]
     blocks = (SIDE, SIDE, SIDE, 16)
-    vmem, anywhere = pl.BlockSpec(memory_space=pltpu.VMEM), pl.BlockSpec(memory_space=pl.ANY)
+    anywhere = pl.BlockSpec(memory_space=pl.ANY)
     return pl.pallas_call(
         layer_kernel,
         out_shape=jax.ShapeDtypeStruct(tokens.shape, BF16),
-        in_specs=[vmem, vmem, vmem, anywhere, anywhere, anywhere],
-        out_specs=vmem,
+        in_specs=[anywhere] * 6,
+        out_specs=anywhere,
         scratch_shapes=[
+            pltpu.VMEM(tokens.shape, BF16),
+            pltpu.VMEM(router.shape[::-1], BF16),
+            pltpu.VMEM(expert_ids.shape[::-1], jnp.int32),
+            pltpu.VMEM(tokens.shape, BF16),
             pltpu.VMEM((ff // (TILE // 2), depth, TILE), BF16),
             pltpu.VMEM((ff, depth), BF16),
             pltpu.VMEM((*blocks, HALF + INFO), BF16),
@@ -508,6 +579,7 @@
             pltpu.VMEM((*blocks, HALF), BF16),
             pltpu.VMEM((*blocks, HALF), BF16),
             *ring_buffers(),
+            pltpu.SemaphoreType.DMA((4,)),
             pltpu.SemaphoreType.DMA((2 * (ff // (TILE // 2)) + 1,)),
             pltpu.SemaphoreType.DMA((8,)),
             pltpu.SemaphoreType.DMA((len(GATHER) * GATHER_SEMS + CHUNKS * SUM_SEMS,)),

time: 75.6 us -> 73.4 us (0.971)
  Pallas kernels: 74 us -> 71.8 us
    pallas_call x1, Pallas kernels: 74 us -> 71.8 us  [layer(): pl.pallas_call(layer_kernel, out_shape=jax.ShapeDtypeStruct(tokens.shape,...]
where the time goes in v5:
time: 73.4 us; the launch traced here: 73.3 us
  Pallas kernels  71.8 us (98%)
  local copies, waits for them, and re-layouts  1.47 us (2%)
    pallas_call x1, Pallas kernels, layer(): pl.pallas_call(layer_kernel, out_shape=jax.ShapeDtypeStruct(tokens.shape,...  71.8 us
    unnamed x1, local copies, waits for them, and re-layouts  1.47 us

profile of v5, /device:TPU:0, one launch (start us, length us, event | category | flops | bytes accessed | tf_op | source)
XLA Modules:
  0.0 73.3 jit_solution(1180493574742149889)
XLA Ops:
  0.0 71.8 %shard_map.64 = bf16[8,4096]{1,0:T(8,128)(2,1)} custom-call(bf16[8,4096]{1,0:T(8,128)(2,1)} %tok_hbm.1, bf16[8,4096]{1,0:T(8,128)(2,1)} %bitcast.2, s32[2,8]{1,0:T(2,128)} %bitcast.3, bf16[1,4096,896]{2,1,0:T(8,128)(2,1)} %gate_hbm.1, bf16[1,4096,896]{2,1,0:T(8,128)(2,1)} %up_hbm.1, bf16[1,896,4096]{2,1,0:T(8,128)(2,1)} %down_hbm.1), custom_call_target="tpu_custom_call" | custom-call | tf_op jit(solution)/shard_map/pallas_call | solution.py:558
  71.8 1.5 %copy.8 = bf16[8,4096]{1,0:T(8,128)(2,1)} copy(bf16[8,4096]{1,0:T(8,128)(2,1)} %shard_map.64) | data formatting | bytes 131072
